TPU v7x, 256 devices: a whole 4x4x8 slice. The times are simulated.
256 devices in a mesh: dom: 256 (over y, z, x, core).
Axes of the slice: x: 4, y: 4, z: 8, core: 2. Of those that a mesh axis runs over, the one named last changes fastest.
Arguments:
- particles: bfloat16 [8192, 2, 7488], P('dom'), may hold values from -6 to 6
- references: bfloat16 [256, 2, 7488], P('dom'), may hold values from -6 to 6
- assignment: int32 [8192, 1], P('dom'), may hold values from 0 to 255
- orientation: int32 [8192], P('dom'), may hold values from 0 to 35
- tilt_range: int32 [2, 8192], P(None, 'dom'), may hold values from 0 to 20
Outputs:
- scores: float32 [8192, 256], P('dom')
- class_means: float32 [256, 2, 7488], P('dom')
- class_load: float32 [256], replicated
Inputs may be any that keep to these rules, and one draw needn't show every extreme that they name: `assignment`: every class has at least one particle.
All inputs are finite; a program needn't handle non-finite values.
Results may differ from a plain program's by a relative error of at most 0.0035.
Values may be sent and summed in bfloat16 or wider, within the bound.
A program may use at most 128 MiB of HBM per device.

v0:
```python
import math

import jax
import jax.numpy as jnp
from jax import lax
from jax.sharding import Mesh
from jax.sharding import PartitionSpec as P

GRID = 24
ORIENTS = 36
COEF = 7488
DOM = ("dom_0", "dom_1", "dom_2", "dom_3")


EPS = 1e-06
GAIN = 6.0
TAU = 0.5
member_rows = 256


def cut_along(shard, dim, size):
    before, after = (shard.shape[:dim], shard.shape[dim + 1 :])
    return jnp.moveaxis(shard.reshape(*before, size, -1, *after), dim, 0)


def summed_on_arrival(shard, axis, dim):
    tiles = cut_along(shard, dim, lax.axis_size(axis))
    arrived = lax.all_to_all(tiles, axis, split_axis=0, concat_axis=0, tiled=True)
    return arrived.astype(jnp.float32).sum(axis=0)


def sum_in_two_steps(shard, axes, dim):
    far, near = axes
    own = summed_on_arrival(cut_along(shard, dim, lax.axis_size(far)), near, dim + 1)
    return jnp.sum(
        lax.all_to_all(own.astype(jnp.bfloat16), far, 0, 0, tiled=True).astype(jnp.float32), axis=0
    )


def tables():
    index = jnp.arange(COEF, dtype=jnp.int32)
    plane = index // (GRID * GRID)
    rest = index % (GRID * GRID)
    col_x = rest // GRID
    col_z = rest % GRID
    freq_x = ((col_x + GRID // 2) % GRID - GRID // 2).astype(jnp.float32)
    freq_y = plane.astype(jnp.float32)
    freq_z = ((col_z + GRID // 2) % GRID - GRID // 2).astype(jnp.float32)
    return (freq_x, freq_y, freq_z)


def wedge_weights(orient, low_bin, high_bin):
    freq_x, freq_y, freq_z = tables()
    angle = orient.astype(jnp.float32) * (2.0 * math.pi / ORIENTS)
    along = -freq_x[None, :] * jnp.sin(angle)[:, None] + freq_y[None, :] * jnp.cos(angle)[:, None]
    radius = along * along + freq_z[None, :] * freq_z[None, :] + 1.0
    cos_two = (along * along - freq_z[None, :] * freq_z[None, :]) / radius
    sin_two = -2.0 * along * freq_z[None, :] / radius
    low = -(40.0 + 1.5 * low_bin.astype(jnp.float32)) * (math.pi / 180.0)
    high = (40.0 + 1.5 * high_bin.astype(jnp.float32)) * (math.pi / 180.0)
    centre = (low + high)[:, None]
    width = (high - low)[:, None]
    return jax.nn.sigmoid(
        GAIN * (cos_two * jnp.cos(centre) + sin_two * jnp.sin(centre) - jnp.cos(width))
    )


def body(particles, references, assignment, orientation, tilt_range):
    part_rows = particles.shape[0]
    coef = particles.shape[2]
    owned = references.shape[0]
    devices = lax.axis_size(DOM)
    classes = owned * devices
    total = part_rows * devices
    cls = assignment[:, 0]
    wedge = wedge_weights(orientation, tilt_range[0], tilt_range[1])
    pf = particles.astype(jnp.float32)
    weighted = (wedge[:, None, :] * pf).astype(jnp.bfloat16)
    flat = weighted.reshape(part_rows, 2 * coef)
    wedge_low = wedge.astype(jnp.bfloat16)
    power = jnp.sum(wedge * (pf[:, 0] * pf[:, 0] + pf[:, 1] * pf[:, 1]), axis=1)
    piece = lax.all_gather(references, DOM, axis=0, tiled=True)
    count = piece.shape[0]
    p32 = piece.astype(jnp.float32)
    ref_power = (p32[:, 0] * p32[:, 0] + p32[:, 1] * p32[:, 1]).astype(jnp.bfloat16)
    intersection = lax.dot_general(
        flat,
        piece.reshape(count, 2 * coef),
        (((1,), (1,)), ((), ())),
        preferred_element_type=jnp.float32,
    )
    energy = lax.dot_general(
        wedge_low, ref_power, (((1,), (1,)), ((), ())), preferred_element_type=jnp.float32
    )
    scores = intersection / (
        math.sqrt(coef) * jnp.sqrt((energy / coef + EPS) * (power[:, None] / coef + EPS))
    )
    ids = lax.iota(jnp.int32, owned * lax.axis_size(DOM))
    onehot = (ids[:, None] == cls[None, :]).astype(jnp.bfloat16)
    numer = sum_in_two_steps(
        jnp.dot(onehot, flat, preferred_element_type=jnp.float32).astype(jnp.bfloat16),
        (("dom_0", "dom_1"), ("dom_2", "dom_3")),
        0,
    )
    labels = jnp.stack([cls, orientation, tilt_range[0], tilt_range[1]])
    every = lax.all_gather(labels, DOM, axis=1, tiled=True)
    class_ids = jnp.arange(classes, dtype=jnp.int32)
    counts = jnp.sum((class_ids[:, None] == every[0][None, :]).astype(jnp.float32), axis=1)
    own_class = lax.axis_index(DOM) * owned + 0
    chosen = every[0] == own_class
    members = jnp.nonzero(chosen, size=total + member_rows, fill_value=0)[0].astype(jnp.int32)
    members_count = jnp.sum(chosen.astype(jnp.int32))
    block_count = (members_count + member_rows - 1) // member_rows

    def member_block(block, acc):
        square_sum, wedge_sum = acc
        first = (block * member_rows).astype(jnp.int32)
        picked = lax.dynamic_slice_in_dim(members, first, member_rows, 0)
        valid = (first + lax.iota(jnp.int32, member_rows) < members_count).astype(jnp.float32)
        member_wedge = wedge_weights(every[1][picked], every[2][picked], every[3][picked])
        squares = (member_wedge * member_wedge).astype(jnp.bfloat16).astype(jnp.float32)
        square_sum = square_sum + jnp.sum(valid[:, None] * squares, axis=0)
        wedge_sum = wedge_sum + jnp.sum(valid * jnp.sum(member_wedge, axis=1))
        return (square_sum, wedge_sum)

    square_sum, wedge_sum = lax.fori_loop(
        0, block_count, member_block, (jnp.zeros((coef,), jnp.float32), jnp.zeros((), jnp.float32))
    )
    denom_rows = [square_sum]
    total_rows = [wedge_sum]
    denom = jnp.stack(denom_rows)
    own_totals = jnp.stack(total_rows)
    bottom = denom + TAU * (own_totals[:, None] / coef + 1.0)
    class_means = numer.reshape(owned, 2, coef) / bottom[:, None, :]
    class_load = counts * classes / total
    return (scores, class_means, class_load)


def solution(mesh):
    split = Mesh(mesh.devices.reshape(4, 8, 4, 2), ("dom_0", "dom_1", "dom_2", "dom_3"))
    placed = (P(DOM, None, None), P(DOM, None, None), P(DOM, None), P(DOM), P(None, DOM))
    return jax.shard_map(
        body,
        mesh=split,
        in_specs=placed,
        out_specs=(P(DOM, None), P(DOM, None, None), P()),
        check_vma=False,
    )
```

profile of v0, /device:TPU:1, one launch (start us, length us, event | category | flops | bytes accessed | tf_op | source)
XLA Modules:
  0.0 330.5 jit_solution(10021585373992793412)
XLA Ops:
  7.4 0.7 fusion.80
  8.1 0.8 cosine_bitcast_fusion.1
  8.9 1.3 copy_convert_fusion
  10.2 1.1 add_divide_fusion.1
  11.3 1.4 multiply_convert_fusion.1
  12.6 0.7 copy.32
  13.4 0.7 reshape.486
  14.1 2.1 fusion.26
  16.3 3.8 %copy.40 = bf16[32,8,1,14976]{3,0,2,1:T(8,128)(2,1)} copy(bf16[32,8,1,14976]{3,1,0,2:T(8,128)(2,1)S(1)} %fusion.26) | data formatting | bytes 15335424 | tf_op jit(solution)/shard_map/reshape;reshape | solution.py:23
  20.1 8.1 %all-to-all-start = ((bf16[8,32,1,14976]{3,1,2,0:T(8,128)(2,1)}), bf16[8,32,1,14976]{3,1,2,0:T(8,128)(2,1)}, u32[]{:S(2)}, u32[]{:S(2)}) async-start(bf16[8,32,1,14976]{3,1,2,0:T(8,128)(2,1)} %bitcast.71), calls=%async_computation | async-start | bytes 15335424 | tf_op jit(solution)/shard_map/all_to_all | solution.py:28
  28.2 0.7 all-gather.3.cloned.1.call-update
  29.0 150.2 %all-gather = s32[256,32,4]{1,2,0:T(4,128)S(1)} all-gather(s32[1,32,4]{1,2,0:T(4,128)S(1)} %add_bitcast_fusion), channel_id=1, replica_groups=mesh['dom_0'=4,'dom_1'=8,'dom_2'=4,'dom_3'=2] {'dom_0','dom_1','dom_2','..., dimensions={0}, use_global_device_ids=true | all-gather | bytes 131584 | tf_op jit(solution)/shard_map/all_gather | solution.py:106
  181.6 57.2 %scatter_custom_fusion = s32[8448]{0:T(1024)S(1)} fusion(s32[8192]{0:T(1024)S(1)} %bitcast.81, s32[8192]{0:T(1024)S(1)} %broadcast.1000, s32[]{:T(128)} %constant.270.clone.1), kind=kCustom, calls=%fused_computation.125 | custom fusion | flops 8192 | bytes 33796 | tf_op jit(solution)/shard_map/scatter-add | solution.py:111
  239.4 0.7 fusion.55
  240.2 4.4 %reduce_sum.94 = bf16[32,14976]{1,0:T(8,128)(2,1)S(1)} reduce(bf16[8,32,1,14976]{3,1,2,0:T(8,128)(2,1)} %all-to-all-done, bf16[]{:T(256)} %constant.286.clone.1), dimensions={0,2}, to_apply=%region_1.2 | reduce | flops 3354624 | bytes 8626178 | tf_op jit(solution)/shard_map/reduce_sum | solution.py:29
  245.1 1.4 reduce.7
  246.5 2.0 reshape.541
  248.5 5.9 %all-to-all-start.1 = ((bf16[32,2,7488]{2,1,0:T(2,128)(2,1)}), bf16[32,2,7488]{2,1,0:T(2,128)(2,1)}, u32[]{:S(2)}, u32[]{:S(2)}) async-start(bf16[32,2,7488]{2,1,0:T(2,128)(2,1)} %reshape.541), calls=%async_computation.1 | async-start | bytes 1933312 | tf_op jit(solution)/shard_map/all_to_all | solution.py:36
  254.5 15.0 %while.15 = (s32[]{:T(128)}, f32[7488]{0:T(1024)S(1)}, f32[]{:T(128)}, s32[]{:T(128)}, s32[]{:T(128)}, /*index=5*/s32[4,8192]{1,0:T(4,128)S(1)}, s32[8448]{0:T(1...) while((s32[]{:T(128)}, f32[7488]{0:T(1024)S(1)}, f32[]{:T(128)}, s32[]{:T(128)}, s32[]{:T(128)}, ...), condition=%wide.region_13.14_spmd, body=%wide.region_9.13_spmd.sunk | while | flops 46529604 | bytes 592063 | solution.py:126
  255.5 1.7 gather_fusion
  257.2 1.7 gather_fusion.1
  259.0 1.7 gather_fusion.2
  260.8 6.5 %fusion.100 = (f32[256]{0:T(256)S(1)}, f32[7488]{0:T(1024)S(1)}) fusion(f32[256]{0:T(256)S(1)} %get-tuple-element.240, f32[256]{0:T(256)S(1)} %sin.43, f32[7488]{0:T(1024)S(1)} %get-tuple-element.242, f32[256]{0:T(256)S(1)} %get-tuple-element.243, f32[7488]{0:T(1024)S(1)} %fusion.97, f32[256]{0:T(256)S(1)} %get-tuple-element.244, ...), kind=kLoop, calls=%fused_computation.7.clone.1 | loop fusion | flops 45998528 | bytes 156928 | tf_op jit(solution)/shard_map/while/body/reduce_sum | solution.py:123
  267.3 1.2 select_reduce_fusion.2
  269.5 1.2 convert_reduce_fusion
  271.3 7.0 %all-to-all-done.1 = bf16[32,2,7488]{2,1,0:T(2,128)(2,1)} async-done(((bf16[32,2,7488]{2,1,0:T(2,128)(2,1)}), bf16[32,2,7488]{2,1,0:T(2,128)(2,1)}, u32[]{:S(2)}, u32[]{:S(2)}) %all-to-all-start.1) | async-done | bytes 958496 | tf_op jit(solution)/shard_map/all_to_all | solution.py:36
  278.3 4.5 %reshape.542 = bf16[32,1,14976]{2,1,0:T(2,128)(2,1)S(1)} reshape(bf16[32,2,7488]{2,1,0:T(2,128)(2,1)} %all-to-all-done.1) | data formatting | bytes 1916928
  282.8 2.0 convert_reduce_fusion.1
  285.5 19.6 %copy.31 = bf16[256,2,7488]{0,2,1:T(8,128)(2,1)} copy(bf16[256,2,7488]{2,1,0:T(2,128)(2,1)} %all-gather.3.cloned.1.call-done) | data formatting | bytes 15335424 | tf_op jit(solution)/shard_map/all_gather | solution.py:82
  305.1 9.9 %convert_element_type.241 = f32[256,2,7488]{0,2,1:T(8,128)} convert(bf16[256,2,7488]{0,2,1:T(8,128)(2,1)} %copy.31) | non-fusion elementwise | flops 3833856 | bytes 23003136 | tf_op jit(solution)/shard_map/convert_element_type | solution.py:84
  315.1 6.5 %fusion.45 = f32[32,256]{1,0:T(8,128)S(1)} fusion(f32[256,2,7488]{0,2,1:T(8,128)} %convert_element_type.241, f32[32]{0:T(128)S(1)} %multiply_add_fusion, f32[32]{0:T(128)S(1)} %get-tuple-element.176, f32[32]{0:T(128)S(1)} %get-tuple-element.175, f32[7488]{0:T(1024)S(1)} %get-tuple-element.180, f32[32]{0:T(128)S(1)} %get-tuple-element.174, ...), kind=kOutput, calls=%fused_computation.71 | convolution fusion | flops 134936576 | bytes 15488768 | tf_op jit(solution)/shard_map/dot_general | solution.py:92
  321.7 2.0 fusion.32
  (51 shorter events, 5.5 us)
Async XLA Ops:
  7.2 7.0 %copy-start = (s32[32,1]{0,1:T(1,128)S(1)}, s32[32,1]{0,1:T(1,128)}, u32[]{:S(2)}) copy-start(s32[32,1]{0,1:T(1,128)} %param.9) | copy-start | bytes 388
  20.1 8.9 %copy-start.1 = (s32[2,32]{1,0:T(2,128)S(1)}, s32[2,32]{1,0:T(2,128)}, u32[]{:S(2)}) copy-start(s32[2,32]{1,0:T(2,128)} %param.11) | copy-start | bytes 772
  20.1 8.9 %copy-start.2 = (s32[32]{0:T(128)S(1)}, s32[32]{0:T(128)}, u32[]{:S(2)}) copy-start(s32[32]{0:T(128)} %param.10) | copy-start | bytes 388
  20.1 220.1 %all-to-all-start = ((bf16[8,32,1,14976]{3,1,2,0:T(8,128)(2,1)}), bf16[8,32,1,14976]{3,1,2,0:T(8,128)(2,1)}, u32[]{:S(2)}, u32[]{:S(2)}) async-start(bf16[8,32,1,14976]{3,1,2,0:T(8,128)(2,1)} %bitcast.71), calls=%async_computation | async-start | bytes 15335424 | tf_op jit(solution)/shard_map/all_to_all | solution.py:28
  28.2 257.3 %all-gather.3.cloned.1.call-start = ((), (), s32[]{:S(2)}) async-start(), calls=%async_computation.2 | async-start | bytes 7763456 | tf_op jit(solution)/shard_map/all_gather | solution.py:82
  248.5 29.8 %all-to-all-start.1 = ((bf16[32,2,7488]{2,1,0:T(2,128)(2,1)}), bf16[32,2,7488]{2,1,0:T(2,128)(2,1)}, u32[]{:S(2)}, u32[]{:S(2)}) async-start(bf16[32,2,7488]{2,1,0:T(2,128)(2,1)} %reshape.541), calls=%async_computation.1 | async-start | bytes 1933312 | tf_op jit(solution)/shard_map/all_to_all | solution.py:36
  305.1 16.5 %slice-start = ((s8[7667712]{0:T(1024)(128)(4,1)}), s8[3473408]{0:T(1024)(128)(4,1)S(1)}, s32[]{:S(2)}) async-start(s8[7667712]{0:T(1024)(128)(4,1)} %bitcast.69), calls=%async_computation.3 | async-start | bytes 6946816
  315.1 6.6 %slice-start.1 = ((s8[7667712]{0:T(1024)(128)(4,1)}), s8[4194304]{0:T(1024)(128)(4,1)S(1)}, s32[]{:S(2)}) async-start(s8[7667712]{0:T(1024)(128)(4,1)} %bitcast.69), calls=%async_computation.4 | async-start | bytes 8388608
Sparse Core Ops, SparseCore 0:
  32.7 132.6 all-gather.2
where the time goes:
time: 334 us; the launch traced here: 331 us
  blocking collectives  150 us (45%)
  other arithmetic  93.9 us (28%)
  local copies, waits for them, and re-layouts  38 us (11%)
  between operations  15 us (4%)
  starting transfers between devices  14.1 us (4%)
  matrix products  10.7 us (3%)
  waiting for transfers between devices  7.69 us (2%)
    all_gather x1, blocking collectives, body(): every = lax.all_gather(labels, DOM, axis=1, tiled=True)  150 us
    scatter-add x1, other arithmetic, body(): jnp.nonzero(chosen, size=total + member_rows, fill_value=0)[0]  57.2 us
    all_gather x1, local copies, waits for them, and re-layouts, body(): piece = lax.all_gather(references, DOM, axis=0, tiled=True)  19.6 us
    convert_element_type x1, other arithmetic, body(): p32 = piece.astype(jnp.float32)  9.95 us
    all_to_all x1, starting transfers between devices, summed_on_arrival(): lax.all_to_all(tiles, axis, split_axis=0, concat_axis=0, tiled=True)  8.14 us
    reduce_sum x2, other arithmetic, member_block(): wedge_sum = wedge_sum + jnp.sum(valid * jnp.sum(member_wedge, axis=1))  7.76 us
    all_to_all x1, waiting for transfers between devices, sum_in_two_steps(): lax.all_to_all(own.astype(jnp.bfloat16), far, 0, 0, tiled=True)  6.98 us
    unnamed x13, local copies, waits for them, and re-layouts  6.88 us
  transfers between devices with their start and end apart: 3, of which 1 were waited for; matrix products, arithmetic and copies ran while one was open for 28% of the time, Pallas kernels for 0%

commit v1 on v0

v1 whole, which is shorter than its diff:
```python
import math

import jax
import jax.numpy as jnp
from jax import lax
from jax.experimental import pallas as pl
from jax.experimental.pallas import tpu as pltpu
from jax.sharding import Mesh
from jax.sharding import PartitionSpec as P

GRID = 24
ORIENTS = 36
COEF = 7488
CLASSES = 256
PARTICLES = 8192
EPS = 1e-06
GAIN = 6.0
TAU = 0.5

NY, NZ, NX, NC = 4, 8, 4, 2
NQ = NY * NX * NC
PART = 32
WIDE = 256
DOM = ("y", "z", "x", "c")
BF = jnp.bfloat16
F32 = jnp.float32


def frequencies(base, lanes=128):
    index = (lax.broadcasted_iota(jnp.int32, (1, lanes), 1) + base).astype(F32)
    plane = jnp.floor((index + 0.5) * (1.0 / (GRID * GRID)))
    rest = index - plane * (GRID * GRID)
    col_x = jnp.floor((rest + 0.5) * (1.0 / GRID))
    col_z = rest - col_x * GRID
    half = GRID // 2
    freq_x = jnp.where(col_x < half, col_x, col_x - GRID)
    freq_z = jnp.where(col_z < half, col_z, col_z - GRID)
    square_z = freq_z * freq_z
    return freq_x, plane, square_z, square_z + 1.0, -2.0 * freq_z, index


def wedge_of(feature, freq):
    sine, cosine, cos_centre, sin_centre, cos_width = feature
    freq_x, freq_y, square_z, square_z1, minus_2z, _ = freq
    along = freq_y * cosine - freq_x * sine
    square = along * along
    turned = ((square - square_z) * cos_centre + (minus_2z * along) * sin_centre) / (square + square_z1)
    return 1.0 / (1.0 + jnp.exp(-GAIN * (turned - cos_width)))


def kernel(
    feat_ref, ref_ref, x_ref,
    score_ref, mean_ref, count_ref,
    fb, r0, xb, stb, c_dummy,
    r1, rr, nb, nr, db, dr, st, zs, s8, tcol,
    pad0, pad1, ft0, ft1, oh, wg, wlow, wsq, wx, rf, rpow,
    sbi, sbe, pbi, pbe, sm, b1, mb,
    f_s, f_r, a_s, a_r, x_s, x_r, t_s, t_r, m_s, m_r,
    rz_s, rz_r, dz_s, dz_r, nz_s, nz_r, sz_s, sz_r,
    pe_s, pe_r, pi_s, pi_r, b_s, b_r,
):
    y = lax.axis_index("y")
    z = lax.axis_index("z")
    x = lax.axis_index("x")
    c = lax.axis_index("c")
    q = y * 8 + x * 2 + c
    chip = y * 4 + x

    def at_plane(t):
        return {"y": t // 8, "z": z, "x": (t // 2) % 4, "c": t % 2}

    def at_z(t):
        return {"y": y, "z": t, "x": x, "c": c}

    def at_chip(t):
        return {"y": t // 4, "z": z, "x": t % 4, "c": c}

    other = {"y": y, "z": z, "x": x, "c": 1 - c}

    def exchange(size, me, place, src, dst, send, recv):
        def copy(t, s):
            return pltpu.make_async_remote_copy(
                src_ref=src(t), dst_ref=dst(s), send_sem=send.at[t], recv_sem=recv.at[s],
                device_id=place(t), device_id_type=pl.DeviceIdType.MESH,
            )

        def start():
            def one(d, _):
                copy((me + d) % size, me).start()
                return 0

            lax.fori_loop(1, size, one, 0)

        def wait_one(d):
            s = (me + size - d) % size
            copy(s, s).wait_recv()
            return s

        def wait_recv():
            def one(d, _):
                wait_one(d)
                return 0

            lax.fori_loop(1, size, one, 0)

        def wait_send():
            def one(d, _):
                copy((me + d) % size, me).wait_send()
                return 0

            lax.fori_loop(1, size, one, 0)

        return start, wait_recv, wait_send, wait_one

    barrier = pltpu.get_barrier_semaphore()

    def greet(d, _):
        pl.semaphore_signal(
            barrier, inc=1, device_id=at_plane((q + d) % NQ), device_id_type=pl.DeviceIdType.MESH
        )
        return 0

    def greet_z(d, _):
        pl.semaphore_signal(
            barrier, inc=1, device_id=at_z((z + d) % NZ), device_id_type=pl.DeviceIdType.MESH
        )
        return 0

    lax.fori_loop(1, NQ, greet, 0)
    lax.fori_loop(1, NZ, greet_z, 0)
    pl.semaphore_wait(barrier, NQ - 1 + NZ - 1)

    feats = exchange(NQ, q, at_plane, lambda t: feat_ref, lambda s: fb.at[s], f_s, f_r)
    refs0 = exchange(NQ, q, at_plane, lambda t: ref_ref.at[t], lambda s: r0.at[s], a_s, a_r)
    parts = exchange(NQ, q, at_plane, lambda t: x_ref.at[t], lambda s: xb.at[s], x_s, x_r)
    stats = exchange(NQ, q, at_plane, lambda t: st, lambda s: stb.at[s], t_s, t_r)
    means = exchange(NQ, q, at_plane, lambda t: mb.at[t], lambda s: mean_ref.at[s], m_s, m_r)
    refsz = exchange(NZ, z, at_z, lambda t: r1, lambda s: rr.at[s], rz_s, rz_r)

    def rows32(t):
        return pl.ds(pl.multiple_of(t * 32, 32), 32)

    denz = exchange(NZ, z, at_z, lambda t: db.at[rows32(t)], lambda s: dr.at[s], dz_s, dz_r)
    numz = exchange(NZ, z, at_z, lambda t: nb.at[:, rows32(t)], lambda s: nr.at[s], nz_s, nz_r)
    statz = exchange(NZ, z, at_z, lambda t: s8, lambda s: zs.at[s], sz_s, sz_r)
    backs = exchange(16, chip, at_chip, lambda t: sm.at[t], lambda s: b1.at[s], b_s, b_r)

    def to_other(src, dst, send, recv):
        return pltpu.make_async_remote_copy(
            src_ref=src.at[:, 1 - c], dst_ref=dst, send_sem=send, recv_sem=recv,
            device_id=other, device_id_type=pl.DeviceIdType.MESH,
        )

    swap_e = to_other(sbe, pbe, pe_s, pe_r)
    swap_i = to_other(sbi, pbi, pi_s, pi_r)

    feats[0]()
    refs0[0]()
    parts[0]()

    fb[pl.ds(q, 1)] = feat_ref[...][None]
    r0[pl.ds(q, 1)] = ref_ref[pl.ds(q, 1)]
    xb[pl.ds(q, 1)] = x_ref[pl.ds(q, 1)]
    pad0[...] = jnp.zeros_like(pad0)
    pad1[...] = jnp.zeros_like(pad1)

    feats[1]()
    pad0[0:32, :] = fb[:, 0, :]
    pad1[0:32, :] = fb[:, 1, :]
    ft0[...] = pad0[...].T
    ft1[...] = pad1[...].T
    class_row = lax.broadcasted_iota(jnp.int32, (CLASSES, 128), 0).astype(F32)
    for tile in range(8):
        row = jnp.sum(fb[4 * tile : 4 * tile + 4, 2, :], axis=0, keepdims=True)
        oh[:, tile * 128 : tile * 128 + 128] = jnp.where(class_row == row, 1.0, 0.0).astype(BF)

    def column(ft, block, lane):
        return jnp.take_along_axis(ft[block * 32 : block * 32 + 32, :], lane, axis=1, mode="promise_in_bounds")

    def features(s):
        lane = jnp.full((32, 128), s, jnp.int32)
        return tuple(column(ft0, k, lane) for k in range(4)) + (column(ft1, 0, lane),)

    mine = [frequencies(q * WIDE), frequencies(q * WIDE + 128)]

    def weigh(s, _):
        feature = features(s)
        for half in range(2):
            wedge = wedge_of(feature, mine[half])
            where = (rows32(s), slice(half * 128, half * 128 + 128))
            wg[where] = wedge
            wlow[where] = wedge.astype(BF)
            wsq[where] = (wedge * wedge).astype(BF)
        return 0

    lax.fori_loop(0, NQ, weigh, 0)

    refs0[1]()
    for part in range(2):
        r1[part] = r0[:, part, :].astype(BF)
    refsz[0]()
    rr[pl.ds(z, 1)] = r1[...][None]

    db[...] = jnp.dot(oh[...], wsq[...], preferred_element_type=F32).astype(BF)
    denz[0]()
    dr[pl.ds(z, 1)] = db[rows32(z)][None]

    own = features(q)

    def own_slice(s, carry):
        power, total = carry
        for half in range(2):
            freq = frequencies(s * WIDE + half * 128)
            wedge = wedge_of(own, freq)
            real = x_ref[s, 0:32, half * 128 : half * 128 + 128].astype(F32)
            imag = x_ref[s, 32:64, half * 128 : half * 128 + 128].astype(F32)
            power = power + wedge * (real * real + imag * imag)
            total = total + jnp.where(freq[5] < COEF, wedge, 0.0)
        return power, total

    nothing = jnp.zeros((32, 128), F32)
    power, total = lax.fori_loop(0, NQ, own_slice, (nothing, nothing))
    power = jnp.sum(power, axis=1, keepdims=True)
    total = jnp.sum(total, axis=1, keepdims=True)
    own_class = column(ft1, 2, jnp.full((32, 128), q, jnp.int32))
    for half in range(2):
        ids = (lax.broadcasted_iota(jnp.int32, (32, 128), 1) + half * 128).astype(F32)
        hit = own_class == ids
        lanes = slice(half * 128, half * 128 + 128)
        st[0:1, lanes] = jnp.sum(jnp.where(hit, 1.0, 0.0), axis=0, keepdims=True)
        st[1:2, lanes] = jnp.sum(jnp.where(hit, total, 0.0), axis=0, keepdims=True)
    stats[0]()
    stb[pl.ds(q, 1)] = st[...][None]

    refsz[1]()
    for part in range(2):
        for plane in range(NZ):
            block = rr[plane, part].astype(F32)
            for k in range(NY):
                rf[part, k * 64 + plane * 8 : k * 64 + plane * 8 + 8, :] = block[8 * k : 8 * k + 8]
    rpow[...] = (rf[0] * rf[0] + rf[1] * rf[1]).astype(BF)
    contract = (((1,), (1,)), ((), ()))
    sbe[...] = lax.dot_general(wlow[...], rpow[...], contract, preferred_element_type=F32).reshape(16, 2, 32, CLASSES)
    swap_e.start()

    def weight(s):
        for part in range(2):
            value = xb[s, 32 * part : 32 * part + 32, :].astype(F32)
            wx[part, rows32(s), :] = (wg[rows32(s), :] * value).astype(BF)

    weight(q)

    def arrive(d, _):
        weight(parts[3](d))
        return 0

    lax.fori_loop(1, NQ, arrive, 0)
    for part in range(2):
        nb[part] = jnp.dot(oh[...], wx[part], preferred_element_type=F32).astype(BF)
    numz[0]()
    nr[pl.ds(z, 1)] = nb[:, rows32(z)][None]

    inter = lax.dot_general(wx[0], rf[0].astype(BF), contract, preferred_element_type=F32)
    inter = inter + lax.dot_general(wx[1], rf[1].astype(BF), contract, preferred_element_type=F32)
    sbi[...] = inter.reshape(16, 2, 32, CLASSES)
    swap_i.start()
    swap_e.wait_recv()
    swap_i.wait_recv()

    def add_core(t, _):
        sm[t, 0] = (sbi[t, c] + pbi[t]).astype(BF)
        sm[t, 1] = (sbe[t, c] + pbe[t]).astype(BF)
        return 0

    lax.fori_loop(0, 16, add_core, 0)
    backs[0]()
    b1[pl.ds(chip, 1)] = sm[pl.ds(chip, 1)]

    stats[1]()
    s8[...] = jnp.sum(stb[...], axis=0)
    statz[0]()
    zs[pl.ds(z, 1)] = s8[...][None]
    statz[1]()
    every = jnp.sum(zs[...], axis=0)
    count_ref[...] = every * (CLASSES / PARTICLES)
    tcol[...] = jnp.zeros_like(tcol)
    tcol[0:2, :] = every
    turned = [tcol[:, 0:128].T, tcol[:, 128:256].T]
    pad0[...] = turned[0]
    pad1[...] = turned[1]

    denz[1]()
    numz[1]()
    denom = jnp.sum(dr[...].astype(F32), axis=0)
    tail = jnp.concatenate(
        [(pad0, pad1)[k // 2][pl.ds(pl.multiple_of((k % 2) * 64 + z * 8, 8), 8), 1:2] for k in range(NY)], axis=0
    )
    bottom = denom + TAU * (tail / COEF + 1.0)
    for part in range(2):
        top = jnp.sum(nr[:, part].astype(F32), axis=0)
        mb[:, part, :] = top / bottom
    means[0]()
    mean_ref[pl.ds(q, 1)] = mb[pl.ds(q, 1)]

    backs[1]()
    inter = jnp.sum(b1[:, 0].astype(F32), axis=0)
    energy = jnp.sum(b1[:, 1].astype(F32), axis=0)
    score_ref[...] = inter / (
        math.sqrt(COEF) * jnp.sqrt((energy / COEF + EPS) * (power / COEF + EPS))
    )
    means[1]()
    for group in (feats, refs0, parts, stats, means, refsz, denz, numz, statz, backs):
        group[2]()
    swap_e.wait_send()
    swap_i.wait_send()


def body(particles, references, assignment, orientation, tilt_range):
    q = lax.axis_index("y") * 8 + lax.axis_index("x") * 2 + lax.axis_index("c")
    padded = NQ * WIDE
    cls = assignment[:, 0]
    angle = orientation.astype(F32) * (2.0 * math.pi / ORIENTS)
    low = -(40.0 + 1.5 * tilt_range[0].astype(F32)) * (math.pi / 180.0)
    high = (40.0 + 1.5 * tilt_range[1].astype(F32)) * (math.pi / 180.0)
    nil = jnp.zeros((PART,), F32)
    in_plane = ((cls // 8) % 8 * 32 + cls // 64 * 8 + cls % 8).astype(F32)
    spot = (jnp.arange(4) == q % 4).astype(F32)
    feat = jnp.stack(
        [
            jnp.concatenate([jnp.sin(angle), jnp.cos(angle), jnp.cos(low + high), jnp.sin(low + high)]),
            jnp.concatenate([jnp.cos(high - low), in_plane, cls.astype(F32), nil]),
            (spot[:, None] * in_plane[None, :]).reshape(128),
            jnp.zeros((128,), F32),
        ]
    )
    refs = jnp.pad(references[0].astype(F32), ((0, 0), (0, padded - COEF)))
    refs = refs.reshape(2, NQ, WIDE).transpose(1, 0, 2)
    xs = jnp.pad(particles, ((0, 0), (0, 0), (0, padded - COEF)))
    xs = xs.reshape(PART, 2, NQ, WIDE).transpose(2, 1, 0, 3).reshape(NQ, 2 * PART, WIDE)

    def v(*shape, dtype=F32):
        return pltpu.VMEM(shape, dtype)

    sem = pltpu.SemaphoreType.DMA
    vm = pl.BlockSpec(memory_space=pltpu.VMEM)
    scores, means, counts = pl.pallas_call(
        kernel,
        out_shape=(
            jax.ShapeDtypeStruct((PART, CLASSES), F32),
            jax.ShapeDtypeStruct((NQ, 2, WIDE), F32),
            jax.ShapeDtypeStruct((2, CLASSES), F32),
        ),
        in_specs=[vm] * 3,
        out_specs=(vm,) * 3,
        scratch_shapes=[
            v(NQ, 4, 128), v(NQ, 2, WIDE), v(NQ, 64, WIDE, dtype=BF), v(NQ, 2, CLASSES), v(8, 128),
            v(2, 32, WIDE, dtype=BF), v(NZ, 2, 32, WIDE, dtype=BF),
            v(2, CLASSES, WIDE, dtype=BF), v(NZ, 2, 32, WIDE, dtype=BF),
            v(CLASSES, WIDE, dtype=BF), v(NZ, 32, WIDE, dtype=BF),
            v(2, CLASSES), v(NZ, 2, CLASSES), v(2, CLASSES), v(128, CLASSES),
            v(128, 128), v(128, 128), v(128, 128), v(128, 128),
            v(CLASSES, 1024, dtype=BF), v(1024, WIDE), v(1024, WIDE, dtype=BF), v(1024, WIDE, dtype=BF),
            v(2, 1024, WIDE, dtype=BF), v(2, CLASSES, WIDE), v(CLASSES, WIDE, dtype=BF),
            v(16, 2, 32, CLASSES), v(16, 2, 32, CLASSES), v(16, 32, CLASSES), v(16, 32, CLASSES),
            v(16, 2, 32, CLASSES, dtype=BF), v(16, 2, 32, CLASSES, dtype=BF), v(NQ, 2, WIDE),
        ] + [sem((NQ,))] * 10 + [sem((NZ,))] * 8 + [sem] * 4 + [sem((16,))] * 2,
        compiler_params=pltpu.CompilerParams(
            collective_id=0, has_side_effects=True, vmem_limit_bytes=48 * 2**20
        ),
    )(feat, refs, xs)
    class_means = means.transpose(1, 0, 2).reshape(1, 2, padded)[:, :, :COEF]
    return scores, class_means, counts[0]


def solution(mesh):
    split = Mesh(mesh.devices.reshape(NY, NZ, NX, NC), DOM)
    placed = (P(DOM, None, None), P(DOM, None, None), P(DOM, None), P(DOM), P(None, DOM))
    return jax.shard_map(
        body,
        mesh=split,
        in_specs=placed,
        out_specs=(P(DOM, None), P(DOM, None, None), P()),
        check_vma=False,
    )
```

time: 334 us -> 60.3 us (0.18)
  blocking collectives: 150 us -> 0 us
  other arithmetic: 93.9 us -> 0.38 us
  Pallas kernels: 0 us -> 51.4 us
  local copies, waits for them, and re-layouts: 38 us -> 7.61 us
  between operations: 15 us -> 0.74 us
  starting transfers between devices: 14.1 us -> 0 us
  matrix products: 10.7 us -> 0 us
  waiting for transfers between devices: 7.69 us -> 0 us
    all_gather x1 -> x0, blocking collectives: 150 us -> none  [body(): every = lax.all_gather(labels, DOM, axis=1, tiled=True)]
    scatter-add x1 -> x0, other arithmetic: 57.2 us -> none  [body(): jnp.nonzero(chosen, size=total + member_rows, fill_value=0)[0]]
    pallas_call x0 -> x1, Pallas kernels: none -> 51.4 us  [body(): pl.pallas_call(kernel, out_shape=(jax.ShapeDtypeStruct((PART, CLASSES), F...]
    all_gather x2 -> x0, local copies, waits for them, and re-layouts: 19.6 us -> none  [the longest x1 19.6 us: body(): piece = lax.all_gather(references, DOM, axis=0, tiled=True)]
    reduce_sum x7 -> x0, other arithmetic: 17.4 us -> none  [the longest x2 7.76 us: member_block(): wedge_sum = wedge_sum + jnp.sum(valid * jnp.sum(member_wedge, axis=1))]
    all_to_all x2 -> x0, starting transfers between devices: 14.1 us -> none  [the longest x1 8.14 us: summed_on_arrival(): lax.all_to_all(tiles, axis, split_axis=0, concat_axis=0, tiled=True)]
    convert_element_type x7 -> x3, other arithmetic: 13.3 us -> 0.03 us  [the longest x1 0.02 us: body(): in_plane = (cls // 8 % 8 * 32 + cls // 64 * 8 + cls % 8).astype(F32)]
    dot_general x3 -> x0, matrix products: 10.7 us -> none  [the longest x1 6.55 us: body(): lax.dot_general(wedge_low, ref_power, (((1,), (1,)), ((), ())), preferred...]
  transfers between devices with their start and end apart: 3 -> 0, of which waited for: 1 -> 0; matrix products, arithmetic and copies ran while one was open for 28% -> 0% of each run, Pallas kernels for 0% -> 0%
where the time goes in v1:
time: 60.3 us; the launch traced here: 60.1 us
  Pallas kernels  51.4 us (85%)
  local copies, waits for them, and re-layouts  7.61 us (13%)
  between operations  0.74 us (1%)
    pallas_call x1, Pallas kernels, body(): pl.pallas_call(kernel, out_shape=(jax.ShapeDtypeStruct((PART, CLASSES), F...  51.4 us
    unnamed x9, local copies, waits for them, and re-layouts  2.65 us
    pad x1, local copies, waits for them, and re-layouts, body(): xs = jnp.pad(particles, ((0, 0), (0, 0), (0, padded - COEF)))  2.29 us
    reshape x2, local copies, waits for them, and re-layouts, body(): xs.reshape(PART, 2, NQ, WIDE).transpose(2, 1, 0, 3)  1.3 us

profile of v1, /device:TPU:1, one launch (start us, length us, event | category | flops | bytes accessed | tf_op | source)
XLA Modules:
  0.0 60.1 jit_solution(6926110102483184294)
XLA Ops:
  0.6 0.0 copy-start.3
  0.7 0.6 %copy-done.3 = s32[32,1]{0,1:T(1,128)S(1)} copy-done((s32[32,1]{0,1:T(1,128)S(1)}, s32[32,1]{0,1:T(1,128)}, u32[]{:S(2)}) %copy-start.3) | copy-done | bytes 152
  1.3 0.1 broadcast_multiply_fusion
  1.4 0.0 copy-start.1
  1.4 0.1 mul.85
  1.5 0.6 copy-done.1
  2.1 0.1 cosine_bitcast_fusion.1
  2.1 0.0 copy-start.2
  2.1 0.6 %copy-done.2 = s32[32]{0:T(128)S(1)} copy-done((s32[32]{0:T(128)S(1)}, s32[32]{0:T(128)}, u32[]{:S(2)}) %copy-start.2) | copy-done | bytes 152
  2.9 0.1 maximum_bitcast_fusion
  2.9 0.1 pad.14.clone
  3.0 0.1 maximum_maximum_fusion.feat_ref
  3.1 2.3 %pad.10 = bf16[32,2,8192]{2,1,0:T(2,128)(2,1)S(1)} pad(bf16[32,2,7488]{2,1,0:T(2,128)(2,1)} %param.5, bf16[]{:T(256)} %constant.91.clone.1), padding=0_0x0_0x0_704 | pad | bytes 2007042 | tf_op jit(solution)/shard_map/jit(_pad)/pad | solution.py:338
  5.4 0.7 %reshape.136 = bf16[32,2,32,256]{3,2,1,0:T(8,128)(2,1)S(1)} reshape(bf16[32,2,8192]{2,1,0:T(2,128)(2,1)S(1)} %pad.10) | data formatting | bytes 2097152 | tf_op jit(solution)/shard_map/reshape | solution.py:339
  6.1 0.0 copy-start
  6.1 0.6 copy.8
  6.7 0.2 copy-done
  6.9 51.4 %shard_map.76 = (f32[32,256]{1,0:T(8,128)S(1)}, f32[32,2,256]{2,1,0:T(2,128)S(1)}, f32[2,256]{1,0:T(2,128)S(1)}) custom-call(f32[4,128]{1,0:T(4,128)S(1)} %maximum_maximum_fusion.feat_ref, f32[32,2,256]{2,1,0:T(2,128)S(1)} %convert_bitcast_fusion.ref_ref, bf16[32,64,256]{2,1,0:T(8,128)(2,1)S(1)} %bitcast.42), custom_call_target="tpu_custom_call" | custom-call | tf_op jit(solution)/shard_map/pallas_call | solution.py:346
  58.3 0.6 %slice.16 = f32[1,2,7488]{2,1,0:T(2,128)} slice(f32[1,2,8192]{2,1,0:T(2,128)S(1)} %bitcast.43), slice={[0:1], [0:2], [0:7488]} | slice | bytes 119808 | tf_op jit(solution)/shard_map/slice | solution.py:371
  58.9 0.6 slice.15
  59.5 0.6 %copy.10 = f32[32,256]{1,0:T(8,128)} copy(f32[32,256]{1,0:T(8,128)S(1)} %get-tuple-element.19) | data formatting | bytes 65536
  (7 shorter events, 0.1 us)
Async XLA Ops:
  0.6 0.7 %copy-start.3 = (s32[32,1]{0,1:T(1,128)S(1)}, s32[32,1]{0,1:T(1,128)}, u32[]{:S(2)}) copy-start(s32[32,1]{0,1:T(1,128)} %param.7) | copy-start | bytes 388
  1.4 0.7 %copy-start.1 = (s32[2,32]{1,0:T(2,128)S(1)}, s32[2,32]{1,0:T(2,128)}, u32[]{:S(2)}) copy-start(s32[2,32]{1,0:T(2,128)} %param.9) | copy-start | bytes 772
  2.1 0.7 %copy-start.2 = (s32[32]{0:T(128)S(1)}, s32[32]{0:T(128)}, u32[]{:S(2)}) copy-start(s32[32]{0:T(128)} %param.8) | copy-start | bytes 388
  6.1 0.8 %copy-start = (bf16[1,2,7488]{2,1,0:T(2,128)(2,1)S(1)}, bf16[1,2,7488]{2,1,0:T(2,128)(2,1)}, u32[]{:S(2)}) copy-start(bf16[1,2,7488]{2,1,0:T(2,128)(2,1)} %param.6) | copy-start | bytes 89860

commit v2 on v1

v2 whole, which is shorter than its diff:
```python
import math

import jax
import jax.numpy as jnp
from jax import lax
from jax.experimental import pallas as pl
from jax.experimental.pallas import tpu as pltpu
from jax.sharding import Mesh
from jax.sharding import PartitionSpec as P

GRID = 24
ORIENTS = 36
COEF = 7488
CLASSES = 256
PARTICLES = 8192
EPS = 1e-06
GAIN = 6.0
TAU = 0.5

NY, NZ, NX, NC = 4, 8, 4, 2
NQ = NY * NX * NC
PART = 32
WIDE = 256
DOM = ("y", "z", "x", "c")
BF = jnp.bfloat16
F32 = jnp.float32


def frequencies(base, lanes=128):
    index = (lax.broadcasted_iota(jnp.int32, (1, lanes), 1) + base).astype(F32)
    plane = jnp.floor((index + 0.5) * (1.0 / (GRID * GRID)))
    rest = index - plane * (GRID * GRID)
    col_x = jnp.floor((rest + 0.5) * (1.0 / GRID))
    col_z = rest - col_x * GRID
    half = GRID // 2
    freq_x = jnp.where(col_x < half, col_x, col_x - GRID)
    freq_z = jnp.where(col_z < half, col_z, col_z - GRID)
    square_z = freq_z * freq_z
    return freq_x, plane, square_z, square_z + 1.0, -2.0 * freq_z, index


def wedge_of(feature, freq):
    sine, cosine, cos_centre, sin_centre, cos_width = feature
    freq_x, freq_y, square_z, square_z1, minus_2z, _ = freq
    along = freq_y * cosine - freq_x * sine
    square = along * along
    turned = ((square - square_z) * cos_centre + (minus_2z * along) * sin_centre) / (square + square_z1)
    return 1.0 / (1.0 + jnp.exp(-GAIN * (turned - cos_width)))


def kernel(
    part_hbm, ref_hbm, cls_hbm, ori_hbm, tilt_hbm,
    score_ref, mean_ref, count_ref,
    raw, rawr, lab_c, lab_o, lab_t, cm, cb, xs, xb, st, stb,
    r1, rr, nb, nr, db, dr, s8, zs, tcol,
    pad0, pad1, ft0, ft1, oh, wg, wlow, wsq, wx, rf, rpow,
    sbi, sbe, pbi, pbe, sm, b1, mb,
    in_s, lab_s, c_s, c_r, x_s, x_r, t_s, t_r, m_s, m_r,
    rz_s, rz_r, dz_s, dz_r, nz_s, nz_r, sz_s, sz_r,
    pe_s, pe_r, pi_s, pi_r, b_s, b_r,
):
    y = lax.axis_index("y")
    z = lax.axis_index("z")
    x = lax.axis_index("x")
    c = lax.axis_index("c")
    q = y * 8 + x * 2 + c
    chip = y * 4 + x

    def at_plane(t):
        return {"y": t // 8, "z": z, "x": (t // 2) % 4, "c": t % 2}

    def at_z(t):
        return {"y": y, "z": t, "x": x, "c": c}

    def at_chip(t):
        return {"y": t // 4, "z": z, "x": t % 4, "c": c}

    other = {"y": y, "z": z, "x": x, "c": 1 - c}

    def over(first, last, step):
        def one(d, _):
            step(d)
            return 0

        lax.fori_loop(first, last, one, 0)

    def exchange(size, me, place, src, dst, blocks, send, recv):
        def start_one(d):
            t = (me + d) % size
            pltpu.make_async_remote_copy(
                src_ref=src(t), dst_ref=dst(me), send_sem=send, recv_sem=recv,
                device_id=place(t), device_id_type=pl.DeviceIdType.MESH,
            ).start()

        def start():
            over(1, size, start_one)

        def wait_recv():
            pltpu.make_async_copy(blocks, blocks, recv).wait()

        def wait_send():
            pltpu.make_async_copy(blocks, blocks, send).wait()

        return start, wait_recv, wait_send

    def rows32(t):
        return pl.ds(pl.multiple_of(t * 32, 32), 32)

    reads = [
        pltpu.make_async_copy(part_hbm, raw, in_s.at[0]),
        pltpu.make_async_copy(ref_hbm, rawr, in_s.at[1]),
        pltpu.make_async_copy(cls_hbm, lab_c, lab_s.at[0]),
        pltpu.make_async_copy(ori_hbm, lab_o, lab_s.at[1]),
        pltpu.make_async_copy(tilt_hbm, lab_t, lab_s.at[2]),
    ]
    for read in reads:
        read.start()

    barrier = pltpu.get_barrier_semaphore()

    def greet(place, me, size):
        def one(d):
            pl.semaphore_signal(
                barrier, inc=1, device_id=place((me + d) % size), device_id_type=pl.DeviceIdType.MESH
            )

        over(1, size, one)

    greet(at_plane, q, NQ)
    greet(at_z, z, NZ)

    few = pl.ds(0, NQ - 1)
    fewz = pl.ds(0, NZ - 1)
    mixed = exchange(NQ, q, at_plane, lambda t: cm.at[t], lambda s: cb.at[s], cb.at[few], c_s, c_r)
    parts = exchange(NQ, q, at_plane, lambda t: xs.at[t], lambda s: xb.at[s], xb.at[few], x_s, x_r)
    stats = exchange(NQ, q, at_plane, lambda t: st, lambda s: stb.at[s], stb.at[few], t_s, t_r)
    means = exchange(NQ, q, at_plane, lambda t: mb.at[t], lambda s: mean_ref.at[s], mb.at[few], m_s, m_r)
    refsz = exchange(NZ, z, at_z, lambda t: r1, lambda s: rr.at[s], rr.at[fewz], rz_s, rz_r)
    denz = exchange(NZ, z, at_z, lambda t: db.at[rows32(t)], lambda s: dr.at[s], dr.at[fewz], dz_s, dz_r)
    numz = exchange(NZ, z, at_z, lambda t: nb.at[:, rows32(t)], lambda s: nr.at[s], nr.at[fewz], nz_s, nz_r)
    statz = exchange(NZ, z, at_z, lambda t: s8, lambda s: zs.at[s], zs.at[fewz], sz_s, sz_r)
    backs = exchange(16, chip, at_chip, lambda t: sm.at[t], lambda s: b1.at[s], b1.at[pl.ds(0, 15)], b_s, b_r)

    def to_other(src, dst, send, recv):
        return pltpu.make_async_remote_copy(
            src_ref=src.at[:, 1 - c], dst_ref=dst, send_sem=send, recv_sem=recv,
            device_id=other, device_id_type=pl.DeviceIdType.MESH,
        )

    swap_e = to_other(sbe, pbe, pe_s, pe_r)
    swap_i = to_other(sbi, pbi, pi_s, pi_r)

    for read in reads[2:]:
        read.wait()
    lane = lax.broadcasted_iota(jnp.int32, (1, 128), 1)
    cls = lab_c[...]
    in_plane = (((cls >> 3) & 7) * 32 + (cls >> 6) * 8 + (cls & 7)).astype(F32)
    angle = lab_o[...].astype(F32) * (2.0 * math.pi / ORIENTS)
    low = -(40.0 + 1.5 * lab_t[0:1, :].astype(F32)) * (math.pi / 180.0)
    high = (40.0 + 1.5 * lab_t[1:2, :].astype(F32)) * (math.pi / 180.0)
    packed = jnp.concatenate([angle, angle, low + high, low + high], axis=1)
    row0 = jnp.where((lane < 32) | (lane >= 96), jnp.sin(packed), jnp.cos(packed))
    row1 = jnp.concatenate([jnp.cos(high - low), in_plane, cls.astype(F32), jnp.zeros((1, 32), F32)], axis=1)
    row2 = jnp.where(lane // 32 == q % 4, jnp.concatenate([in_plane] * 4, axis=1), 0.0)
    cm[:, 2:3, 0:128] = jnp.broadcast_to(row0[None], (NQ, 1, 128))
    cm[:, 2:3, 128:256] = jnp.broadcast_to(row1[None], (NQ, 1, 128))
    cm[:, 3:4, 0:128] = jnp.broadcast_to(row2[None], (NQ, 1, 128))
    cm[:, 3:4, 128:256] = jnp.zeros((NQ, 1, 128), F32)
    reads[1].wait()
    whole = COEF // WIDE
    rest = COEF - whole * WIDE
    for t in range(NQ):
        if t < whole:
            cm[t, 0:2, :] = rawr[0, :, t * WIDE : (t + 1) * WIDE].astype(F32)
        else:
            cm[t, 0:2, :] = jnp.zeros((2, WIDE), F32)
    cm[whole, 0:2, 0:rest] = rawr[0, :, whole * WIDE : COEF].astype(F32)

    reads[0].wait()

    def relay(t):
        block = raw[:, :, pl.ds(pl.multiple_of(t * WIDE, WIDE), WIDE)]
        xs[t] = jnp.swapaxes(block, 0, 1).reshape(2 * PART, WIDE)

    over(0, whole, relay)
    for t in range(whole, NQ):
        xs[t] = jnp.zeros((2 * PART, WIDE), BF)
    xs[whole, :, 0:rest] = jnp.swapaxes(raw[:, :, whole * WIDE : COEF], 0, 1).reshape(2 * PART, rest)
    pl.semaphore_wait(barrier, NQ - 1 + NZ - 1)

    mixed[0]()
    parts[0]()
    cb[pl.ds(q, 1)] = cm[pl.ds(q, 1)]
    xb[pl.ds(q, 1)] = xs[pl.ds(q, 1)]

    def column(ft, block, index):
        return jnp.take_along_axis(ft[block * 32 : block * 32 + 32, :], index, axis=1, mode="promise_in_bounds")

    def features(s):
        index = jnp.full((32, 128), s, jnp.int32)
        return tuple(column(ft0, k, index) for k in range(4)) + (column(ft1, 0, index),)

    pad0[...] = jnp.broadcast_to(row0, (128, 128))
    pad1[...] = jnp.broadcast_to(row1, (128, 128))
    ft0[...] = pad0[...].T
    ft1[...] = pad1[...].T
    own = tuple(ft0[k * 32 : k * 32 + 32, :] for k in range(4)) + (ft1[0:32, :],)
    own_class = ft1[64:96, :]

    def own_slice(s, carry):
        power, total = carry
        for half in range(2):
            freq = frequencies(s * WIDE + half * 128)
            wedge = wedge_of(own, freq)
            real = xs[s, 0:32, half * 128 : half * 128 + 128].astype(F32)
            imag = xs[s, 32:64, half * 128 : half * 128 + 128].astype(F32)
            power = power + wedge * (real * real + imag * imag)
            total = total + jnp.where(freq[5] < COEF, wedge, 0.0)
        return power, total

    nothing = jnp.zeros((32, 128), F32)
    power, total = lax.fori_loop(0, NQ, own_slice, (nothing, nothing))
    power = jnp.sum(power, axis=1, keepdims=True)
    total = jnp.sum(total, axis=1, keepdims=True)
    for half in range(2):
        ids = (lax.broadcasted_iota(jnp.int32, (32, 128), 1) + half * 128).astype(F32)
        hit = own_class == ids
        lanes = slice(half * 128, half * 128 + 128)
        st[0:1, lanes] = jnp.sum(jnp.where(hit, 1.0, 0.0), axis=0, keepdims=True)
        st[1:2, lanes] = jnp.sum(jnp.where(hit, total, 0.0), axis=0, keepdims=True)
    stats[0]()
    stb[pl.ds(q, 1)] = st[...][None]

    mixed[1]()
    for part in range(2):
        r1[part] = cb[:, part, :].astype(BF)
    refsz[0]()
    rr[pl.ds(z, 1)] = r1[...][None]

    pad0[0:32, :] = cb[:, 2, 0:128]
    pad1[0:32, :] = cb[:, 2, 128:256]
    ft0[...] = pad0[...].T
    ft1[...] = pad1[...].T
    class_row = lax.broadcasted_iota(jnp.int32, (CLASSES, 128), 0).astype(F32)
    for tile in range(8):
        row = jnp.sum(cb[4 * tile : 4 * tile + 4, 3, 0:128], axis=0, keepdims=True)
        oh[:, tile * 128 : tile * 128 + 128] = jnp.where(class_row == row, 1.0, 0.0).astype(BF)

    mine = [frequencies(q * WIDE), frequencies(q * WIDE + 128)]

    def weigh(s):
        feature = features(s)
        for half in range(2):
            wedge = wedge_of(feature, mine[half])
            where = (rows32(s), slice(half * 128, half * 128 + 128))
            wg[where] = wedge
            wlow[where] = wedge.astype(BF)
            wsq[where] = (wedge * wedge).astype(BF)

    over(0, NQ, weigh)

    db[...] = jnp.dot(oh[...], wsq[...], preferred_element_type=F32).astype(BF)
    denz[0]()
    dr[pl.ds(z, 1)] = db[rows32(z)][None]

    refsz[1]()
    for part in range(2):
        for plane in range(NZ):
            block = rr[plane, part].astype(F32)
            for k in range(NY):
                rf[part, k * 64 + plane * 8 : k * 64 + plane * 8 + 8, :] = block[8 * k : 8 * k + 8]
    rpow[...] = (rf[0] * rf[0] + rf[1] * rf[1]).astype(BF)
    contract = (((1,), (1,)), ((), ()))
    sbe[...] = lax.dot_general(wlow[...], rpow[...], contract, preferred_element_type=F32).reshape(16, 2, 32, CLASSES)
    swap_e.start()

    parts[1]()
    stats[1]()
    s8[...] = jnp.sum(stb[...], axis=0)
    statz[0]()
    zs[pl.ds(z, 1)] = s8[...][None]

    def weight(s):
        for part in range(2):
            value = xb[s, 32 * part : 32 * part + 32, :].astype(F32)
            wx[part, rows32(s), :] = (wg[rows32(s), :] * value).astype(BF)

    over(0, NQ, weight)
    inter = lax.dot_general(wx[0], rf[0].astype(BF), contract, preferred_element_type=F32)
    inter = inter + lax.dot_general(wx[1], rf[1].astype(BF), contract, preferred_element_type=F32)
    sbi[...] = inter.reshape(16, 2, 32, CLASSES)
    swap_i.start()
    for part in range(2):
        nb[part] = jnp.dot(oh[...], wx[part], preferred_element_type=F32).astype(BF)
    numz[0]()
    nr[pl.ds(z, 1)] = nb[:, rows32(z)][None]

    swap_e.wait_recv()
    swap_i.wait_recv()

    def add_core(t):
        sm[t, 0] = (sbi[t, c] + pbi[t]).astype(BF)
        sm[t, 1] = (sbe[t, c] + pbe[t]).astype(BF)

    over(0, 16, add_core)
    backs[0]()
    b1[pl.ds(chip, 1)] = sm[pl.ds(chip, 1)]

    statz[1]()
    every = jnp.sum(zs[...], axis=0)
    count_ref[...] = every * (CLASSES / PARTICLES)
    tcol[...] = jnp.zeros_like(tcol)
    tcol[0:2, :] = every
    turned = [tcol[:, 0:128].T, tcol[:, 128:256].T]
    pad0[...] = turned[0]
    pad1[...] = turned[1]

    denz[1]()
    denom = jnp.sum(dr[...].astype(F32), axis=0)
    tail = jnp.concatenate(
        [(pad0, pad1)[k // 2][pl.ds(pl.multiple_of((k % 2) * 64 + z * 8, 8), 8), 1:2] for k in range(NY)], axis=0
    )
    bottom = denom + TAU * (tail / COEF + 1.0)
    numz[1]()
    for part in range(2):
        top = jnp.sum(nr[:, part].astype(F32), axis=0)
        mb[:, part, :] = top / bottom
    means[0]()
    mean_ref[pl.ds(q, 1)] = mb[pl.ds(q, 1)]

    backs[1]()
    inter = jnp.sum(b1[:, 0].astype(F32), axis=0)
    energy = jnp.sum(b1[:, 1].astype(F32), axis=0)
    score_ref[...] = inter / (
        math.sqrt(COEF) * jnp.sqrt((energy / COEF + EPS) * (power / COEF + EPS))
    )
    means[1]()
    for group in (mixed, parts, stats, means, refsz, denz, numz, statz, backs):
        group[2]()
    swap_e.wait_send()
    swap_i.wait_send()


def body(particles, references, assignment, orientation, tilt_range):
    padded = NQ * WIDE

    def v(*shape, dtype=F32):
        return pltpu.VMEM(shape, dtype)

    sem = pltpu.SemaphoreType.DMA
    vm = pl.BlockSpec(memory_space=pltpu.VMEM)
    anywhere = pl.BlockSpec(memory_space=pl.ANY)
    scores, means, counts = pl.pallas_call(
        kernel,
        out_shape=(
            jax.ShapeDtypeStruct((PART, CLASSES), F32),
            jax.ShapeDtypeStruct((NQ, 2, WIDE), F32),
            jax.ShapeDtypeStruct((2, CLASSES), F32),
        ),
        in_specs=[anywhere] * 5,
        out_specs=(vm,) * 3,
        scratch_shapes=[
            v(PART, 2, COEF, dtype=BF), v(1, 2, COEF, dtype=BF),
            v(1, PART, dtype=jnp.int32), v(1, PART, dtype=jnp.int32), v(2, PART, dtype=jnp.int32),
            v(NQ, 4, WIDE), v(NQ, 4, WIDE), v(NQ, 64, WIDE, dtype=BF), v(NQ, 64, WIDE, dtype=BF),
            v(2, CLASSES), v(NQ, 2, CLASSES),
            v(2, 32, WIDE, dtype=BF), v(NZ, 2, 32, WIDE, dtype=BF),
            v(2, CLASSES, WIDE, dtype=BF), v(NZ, 2, 32, WIDE, dtype=BF),
            v(CLASSES, WIDE, dtype=BF), v(NZ, 32, WIDE, dtype=BF),
            v(2, CLASSES), v(NZ, 2, CLASSES), v(128, CLASSES),
            v(128, 128), v(128, 128), v(128, 128), v(128, 128),
            v(CLASSES, 1024, dtype=BF), v(1024, WIDE), v(1024, WIDE, dtype=BF), v(1024, WIDE, dtype=BF),
            v(2, 1024, WIDE, dtype=BF), v(2, CLASSES, WIDE), v(CLASSES, WIDE, dtype=BF),
            v(16, 2, 32, CLASSES), v(16, 2, 32, CLASSES), v(16, 32, CLASSES), v(16, 32, CLASSES),
            v(16, 2, 32, CLASSES, dtype=BF), v(16, 2, 32, CLASSES, dtype=BF), v(NQ, 2, WIDE),
            sem((2,)), sem((3,)),
        ] + [sem] * 22,
        compiler_params=pltpu.CompilerParams(
            collective_id=0, has_side_effects=True, vmem_limit_bytes=48 * 2**20
        ),
    )(particles, references, assignment.T, orientation[None], tilt_range)
    class_means = means.transpose(1, 0, 2).reshape(1, 2, padded)[:, :, :COEF]
    return scores, class_means, counts[0]


def solution(mesh):
    split = Mesh(mesh.devices.reshape(NY, NZ, NX, NC), DOM)
    placed = (P(DOM, None, None), P(DOM, None, None), P(DOM, None), P(DOM), P(None, DOM))
    return jax.shard_map(
        body,
        mesh=split,
        in_specs=placed,
        out_specs=(P(DOM, None), P(DOM, None, None), P()),
        check_vma=False,
    )
```

time: 60.3 us -> 52.8 us (0.88)
  Pallas kernels: 51.4 us -> 47.5 us
  local copies, waits for them, and re-layouts: 7.61 us -> 4.43 us
    pallas_call x1, Pallas kernels: 51.4 us -> 47.5 us  [body(): pl.pallas_call(kernel, out_shape=(jax.ShapeDtypeStruct((PART, CLASSES), F...]
    pad x2 -> x0, local copies, waits for them, and re-layouts: 2.31 us -> none  [the longest x1 2.29 us: body(): xs = jnp.pad(particles, ((0, 0), (0, 0), (0, padded - COEF)))]
    reshape x2 -> x0, local copies, waits for them, and re-layouts: 1.3 us -> none  [body(): xs.reshape(PART, 2, NQ, WIDE).transpose(2, 1, 0, 3)]
    unnamed x9 -> x11, local copies, waits for them, and re-layouts: 2.65 us -> 3.23 us
where the time goes in v2:
time: 52.8 us; the launch traced here: 52.6 us
  Pallas kernels  47.5 us (90%)
  local copies, waits for them, and re-layouts  4.43 us (8%)
  between operations  0.67 us (1%)
    pallas_call x1, Pallas kernels, body(): pl.pallas_call(kernel, out_shape=(jax.ShapeDtypeStruct((PART, CLASSES), F...  47.5 us
    unnamed x11, local copies, waits for them, and re-layouts  3.23 us

profile of v2, /device:TPU:1, one launch (start us, length us, event | category | flops | bytes accessed | tf_op | source)
XLA Modules:
  0.0 52.6 jit_solution(17416019844174105875)
XLA Ops:
  0.6 0.0 copy-start.4
  0.6 0.0 copy-start.2
  0.7 0.0 copy-start.3
  0.7 0.6 %copy-done.4 = s32[32]{0:T(128)S(1)} copy-done((s32[32]{0:T(128)S(1)}, s32[32]{0:T(128)}, u32[]{:S(2)}) %copy-start.4) | copy-done | bytes 152
  1.3 0.0 copy-done.2
  1.3 0.0 copy-done.3
  1.3 0.0 copy-start
  1.3 1.2 %copy-done = bf16[32,2,7488]{2,1,0:T(2,128)(2,1)S(1)} copy-done((bf16[32,2,7488]{2,1,0:T(2,128)(2,1)S(1)}, bf16[32,2,7488]{2,1,0:T(2,128)(2,1)}, u32[]{:S(2)}) %copy-start) | copy-done | bytes 958488
  2.5 0.0 copy-start.1
  2.5 0.7 %copy-done.1 = bf16[1,2,7488]{2,1,0:T(2,128)(2,1)S(1)} copy-done((bf16[1,2,7488]{2,1,0:T(2,128)(2,1)S(1)}, bf16[1,2,7488]{2,1,0:T(2,128)(2,1)}, u32[]{:S(2)}) %copy-start.1) | copy-done | bytes 29976
  3.3 47.5 %shard_map.76 = (f32[32,256]{1,0:T(8,128)S(1)}, f32[32,2,256]{2,1,0:T(2,128)S(1)}, f32[2,256]{1,0:T(2,128)S(1)}) custom-call(bf16[32,2,7488]{2,1,0:T(2,128)(2,1)S(1)} %copy-done, bf16[1,2,7488]{2,1,0:T(2,128)(2,1)S(1)} %copy-done.1, s32[1,32]{1,0:T(1,128)S(1)} %bitcast.7, s32[1,32]{1,0:T(1,128)S(1)} %bitcast.8, s32[2,32]{1,0:T(2,128)S(1)} %copy-done.2), custom_call_target="tpu_custom_call" | custom-call | tf_op jit(solution)/shard_map/pallas_call | solution.py:353
  50.7 0.6 %slice.8 = f32[1,2,7488]{2,1,0:T(2,128)} slice(f32[1,2,8192]{2,1,0:T(2,128)S(1)} %bitcast.6), slice={[0:1], [0:2], [0:7488]} | slice | bytes 119808 | tf_op jit(solution)/shard_map/slice | solution.py:382
  51.4 0.6 %slice.7 = f32[1,256]{1,0:T(1,128)} slice(f32[2,256]{1,0:T(2,128)S(1)} %get-tuple-element.8), slice={[0:1], [0:256]} | slice | bytes 2048 | tf_op jit(solution)/shard_map/slice | solution.py:383
  51.9 0.6 %copy.9 = f32[32,256]{1,0:T(8,128)} copy(f32[32,256]{1,0:T(8,128)S(1)} %get-tuple-element.12) | data formatting | bytes 65536
Async XLA Ops:
  0.6 0.7 %copy-start.4 = (s32[32]{0:T(128)S(1)}, s32[32]{0:T(128)}, u32[]{:S(2)}) copy-start(s32[32]{0:T(128)} %param.8) | copy-start | bytes 388
  0.6 0.7 %copy-start.2 = (s32[2,32]{1,0:T(2,128)S(1)}, s32[2,32]{1,0:T(2,128)}, u32[]{:S(2)}) copy-start(s32[2,32]{1,0:T(2,128)} %tilt_hbm.1) | copy-start | bytes 772
  0.7 0.7 %copy-start.3 = (s32[32,1]{0,1:T(1,128)S(1)}, s32[32,1]{0,1:T(1,128)}, u32[]{:S(2)}) copy-start(s32[32,1]{0,1:T(1,128)} %param.7) | copy-start | bytes 388
  1.3 1.2 %copy-start = (bf16[32,2,7488]{2,1,0:T(2,128)(2,1)S(1)}, bf16[32,2,7488]{2,1,0:T(2,128)(2,1)}, u32[]{:S(2)}) copy-start(bf16[32,2,7488]{2,1,0:T(2,128)(2,1)} %part_hbm.1) | copy-start | bytes 2875396
  2.5 0.8 %copy-start.1 = (bf16[1,2,7488]{2,1,0:T(2,128)(2,1)S(1)}, bf16[1,2,7488]{2,1,0:T(2,128)(2,1)}, u32[]{:S(2)}) copy-start(bf16[1,2,7488]{2,1,0:T(2,128)(2,1)} %ref_hbm.1) | copy-start | bytes 89860

commit v3 on v2

v3 whole, which is shorter than its diff:
```python
import math

import jax
import jax.numpy as jnp
from jax import lax
from jax.experimental import pallas as pl
from jax.experimental.pallas import tpu as pltpu
from jax.sharding import Mesh
from jax.sharding import PartitionSpec as P

GRID = 24
ORIENTS = 36
COEF = 7488
CLASSES = 256
PARTICLES = 8192
EPS = 1e-06
GAIN = 6.0
TAU = 0.5

NY, NZ, NX, NC = 4, 8, 4, 2
NQ = NY * NX * NC
PART = 32
WIDE = 256
DOM = ("y", "z", "x", "c")
BF = jnp.bfloat16
F32 = jnp.float32


def frequencies(base, lanes=128):
    index = (lax.broadcasted_iota(jnp.int32, (1, lanes), 1) + base).astype(F32)
    plane = jnp.floor((index + 0.5) * (1.0 / (GRID * GRID)))
    rest = index - plane * (GRID * GRID)
    col_x = jnp.floor((rest + 0.5) * (1.0 / GRID))
    col_z = rest - col_x * GRID
    half = GRID // 2
    freq_x = jnp.where(col_x < half, col_x, col_x - GRID)
    freq_z = jnp.where(col_z < half, col_z, col_z - GRID)
    square_z = freq_z * freq_z
    return freq_x, plane, square_z, square_z + 1.0, -2.0 * freq_z, index


def wedge_of(feature, freq):
    sine, cosine, cos_centre, sin_centre, cos_width = feature
    freq_x, freq_y, square_z, square_z1, minus_2z, _ = freq
    along = freq_y * cosine - freq_x * sine
    square = along * along
    turned = ((square - square_z) * cos_centre + (minus_2z * along) * sin_centre) / (square + square_z1)
    return 1.0 / (1.0 + jnp.exp(-GAIN * (turned - cos_width)))


def kernel(
    part_hbm, ref_hbm, cls_hbm, ori_hbm, tilt_hbm,
    score_ref, mean_ref, count_ref,
    raw, rawr, lab_c, lab_o, lab_t, cm, cb, xs, xb, st, stb,
    r1, rr, nb, nr, db, dr, s8, zs, tcol,
    pad0, pad1, ft, sel, oh, wg, wlow, wsq, wx, rf, rpow,
    sbi, sbe, pbi, pbe, sm, b1, mb, mr,
    in_s, lab_s, x_s, x_r, nz_s, nz_r, c_s, c_r, t_s, t_r, m_s, m_r,
    rz_s, rz_r, dz_s, dz_r, sz_s, sz_r,
    pe_s, pe_r, pi_s, pi_r, b_s, b_r,
):
    y = lax.axis_index("y")
    z = lax.axis_index("z")
    x = lax.axis_index("x")
    c = lax.axis_index("c")
    q = y * 8 + x * 2 + c
    chip = y * 4 + x

    def at_plane(t):
        return {"y": t // 8, "z": z, "x": (t // 2) % 4, "c": t % 2}

    def at_z(t):
        return {"y": y, "z": t, "x": x, "c": c}

    def at_chip(t):
        return {"y": t // 4, "z": z, "x": t % 4, "c": c}

    other = {"y": y, "z": z, "x": x, "c": 1 - c}

    def over(first, last, step):
        def one(d, _):
            step(d)
            return 0

        lax.fori_loop(first, last, one, 0)

    def exchange(size, me, place, src, dst, blocks, send, recv):
        def start_one(d):
            t = (me + d) % size
            pltpu.make_async_remote_copy(
                src_ref=src(t), dst_ref=dst(me), send_sem=send, recv_sem=recv,
                device_id=place(t), device_id_type=pl.DeviceIdType.MESH,
            ).start()

        def start():
            over(1, size, start_one)

        def wait_recv():
            pltpu.make_async_copy(blocks, blocks, recv).wait()

        def wait_send():
            pltpu.make_async_copy(blocks, blocks, send).wait()

        return start, wait_recv, wait_send

    def rows32(t):
        return pl.ds(pl.multiple_of(t * 32, 32), 32)

    barrier = pltpu.get_barrier_semaphore()

    def greet(place, me, size):
        def one(d):
            pl.semaphore_signal(
                barrier, inc=1, device_id=place((me + d) % size), device_id_type=pl.DeviceIdType.MESH
            )

        over(1, size, one)

    greet(at_plane, q, NQ)
    greet(at_z, z, NZ)

    reads = [
        pltpu.make_async_copy(part_hbm, raw, in_s.at[0]),
        pltpu.make_async_copy(ref_hbm, rawr, in_s.at[1]),
        pltpu.make_async_copy(cls_hbm, lab_c, lab_s.at[0]),
        pltpu.make_async_copy(ori_hbm, lab_o, lab_s.at[1]),
        pltpu.make_async_copy(tilt_hbm, lab_t, lab_s.at[2]),
    ]
    for read in reads:
        read.start()

    few = pl.ds(0, NQ - 1)
    fewz = pl.ds(0, NZ - 1)
    mixed = exchange(NQ, q, at_plane, lambda t: cm.at[t], lambda s: cb.at[s], cb.at[few], c_s, c_r)

    def parts_of(h):
        return exchange(
            NQ, q, at_plane, lambda t: xs.at[h, t], lambda s: xb.at[h, s], xb.at[h, few], x_s.at[h], x_r.at[h]
        )

    parts = [parts_of(0), parts_of(1)]
    stats = exchange(NQ, q, at_plane, lambda t: st, lambda s: stb.at[s], stb.at[few], t_s, t_r)
    means = exchange(NQ, q, at_plane, lambda t: mb.at[t], lambda s: mr.at[s], mr.at[few], m_s, m_r)
    refsz = exchange(NZ, z, at_z, lambda t: r1, lambda s: rr.at[s], rr.at[fewz], rz_s, rz_r)
    denz = exchange(NZ, z, at_z, lambda t: db.at[rows32(t)], lambda s: dr.at[s], dr.at[fewz], dz_s, dz_r)

    def numz_of(h):
        return exchange(
            NZ, z, at_z, lambda t: nb.at[h, rows32(t)], lambda s: nr.at[h, s], nr.at[h, fewz], nz_s.at[h], nz_r.at[h]
        )

    numz = [numz_of(0), numz_of(1)]
    statz = exchange(NZ, z, at_z, lambda t: s8, lambda s: zs.at[s], zs.at[fewz], sz_s, sz_r)
    backs = exchange(16, chip, at_chip, lambda t: sm.at[t], lambda s: b1.at[s], b1.at[pl.ds(0, 15)], b_s, b_r)

    def to_other(src, dst, send, recv):
        return pltpu.make_async_remote_copy(
            src_ref=src.at[:, 1 - c], dst_ref=dst, send_sem=send, recv_sem=recv,
            device_id=other, device_id_type=pl.DeviceIdType.MESH,
        )

    swap_e = to_other(sbe, pbe, pe_s, pe_r)
    swap_i = to_other(sbi, pbi, pi_s, pi_r)

    for read in reads[2:]:
        read.wait()
    labels = jnp.concatenate([lab_c[...], lab_o[...], lab_t[0:1, :], lab_t[1:2, :]], axis=1).astype(F32)
    pair = jnp.concatenate([labels, jnp.zeros((1, 128), F32)], axis=0).astype(BF)
    cm[:, 2:4, 0:128] = jnp.broadcast_to(pair[None], (NQ, 2, 128))
    cm[:, 2:4, 128:256] = jnp.zeros((NQ, 2, 128), BF)
    reads[1].wait()
    whole = COEF // WIDE
    rest = COEF - whole * WIDE
    for t in range(NQ):
        if t < whole:
            cm[t, 0:2, :] = rawr[0, :, t * WIDE : (t + 1) * WIDE]
        else:
            cm[t, 0:2, :] = jnp.zeros((2, WIDE), BF)
    cm[whole, 0:2, 0:rest] = rawr[0, :, whole * WIDE : COEF]

    reads[0].wait()

    def relay(t):
        for h in range(2):
            block = raw[:, :, pl.ds(pl.multiple_of(t * WIDE + h * 128, 128), 128)]
            both = jnp.swapaxes(block, 0, 1)
            xs[h, t, :, 0:128] = both[0]
            xs[h, t, :, 128:256] = both[1]

    over(0, whole, relay)
    for h in range(2):
        for t in range(whole, NQ):
            xs[h, t] = jnp.zeros((PART, WIDE), BF)
    both = jnp.swapaxes(raw[:, :, whole * WIDE : COEF], 0, 1)
    xs[0, whole, :, 0:rest] = both[0]
    xs[0, whole, :, 128 : 128 + rest] = both[1]
    pl.semaphore_wait(barrier, NQ - 1 + NZ - 1)

    mixed[0]()
    parts[0][0]()
    parts[1][0]()
    cb[pl.ds(q, 1)] = cm[pl.ds(q, 1)]
    for h in range(2):
        xb[h, pl.ds(q, 1)] = xs[h, pl.ds(q, 1)]

    def features_of(turned):
        angle = turned[32:64] * (2.0 * math.pi / ORIENTS)
        low = -(40.0 + 1.5 * turned[64:96]) * (math.pi / 180.0)
        high = (40.0 + 1.5 * turned[96:128]) * (math.pi / 180.0)
        centre = low + high
        return jnp.sin(angle), jnp.cos(angle), jnp.cos(centre), jnp.sin(centre), jnp.cos(high - low)

    pad0[...] = jnp.broadcast_to(labels, (128, 128))
    turned = pad0[...].T
    own = features_of(turned)
    own_class = turned[0:32]

    def own_slice(s, carry):
        power, total = carry
        for half in range(2):
            freq = frequencies(s * WIDE + half * 128)
            wedge = wedge_of(own, freq)
            real = xs[half, s, :, 0:128].astype(F32)
            imag = xs[half, s, :, 128:256].astype(F32)
            power = power + wedge * (real * real + imag * imag)
            total = total + jnp.where(freq[5] < COEF, wedge, 0.0)
        return power, total

    nothing = jnp.zeros((32, 128), F32)
    power, total = lax.fori_loop(0, NQ, own_slice, (nothing, nothing))
    power = jnp.sum(power, axis=1, keepdims=True)
    total = jnp.sum(total, axis=1, keepdims=True)
    for half in range(2):
        ids = (lax.broadcasted_iota(jnp.int32, (32, 128), 1) + half * 128).astype(F32)
        hit = own_class == ids
        lanes = slice(half * 128, half * 128 + 128)
        st[0:1, lanes] = jnp.sum(jnp.where(hit, 1.0, 0.0), axis=0, keepdims=True)
        st[1:2, lanes] = jnp.sum(jnp.where(hit, total, 0.0), axis=0, keepdims=True)
    stats[0]()
    stb[pl.ds(q, 1)] = st[...][None]

    mixed[1]()
    both = jnp.swapaxes(cb[:, 0:2, :], 0, 1)
    for h in range(2):
        for part in range(2):
            at = h * 256 + part * 128
            r1[:, at : at + 128] = both[part, :, h * 128 : h * 128 + 128]
    refsz[0]()
    rr[pl.ds(z, 1)] = r1[...][None]

    every = jnp.swapaxes(cb[:, 2:4, 0:128], 0, 1)[0].astype(F32)
    pad0[0:32, :] = every
    for k, feature in enumerate(features_of(pad0[...].T)):
        ft[k] = feature
    sub = lax.broadcasted_iota(jnp.int32, (32, 128), 0)
    cls = jnp.where(lax.broadcasted_iota(jnp.int32, (32, 128), 1) < 32, every, 0.0).astype(jnp.int32)
    in_plane = (((cls >> 3) & 7) * 32 + (cls >> 6) * 8 + (cls & 7)).astype(F32)
    chosen = in_plane
    for k in range(1, 4):
        chosen = jnp.where((sub & 3) == k, pltpu.roll(in_plane, 32 * k, 1), chosen)
    sel[...] = chosen
    class_row = lax.broadcasted_iota(jnp.int32, (CLASSES, 128), 0).astype(F32)
    for tile in range(8):
        row = jnp.sum(sel[4 * tile : 4 * tile + 4, :], axis=0, keepdims=True)
        oh[:, tile * 128 : tile * 128 + 128] = jnp.where(class_row == row, 1.0, 0.0).astype(BF)

    def features(s):
        index = jnp.full((32, 128), s, jnp.int32)
        return tuple(jnp.take_along_axis(ft[k], index, axis=1, mode="promise_in_bounds") for k in range(5))

    mine = [frequencies(q * WIDE), frequencies(q * WIDE + 128)]

    def weigh(s):
        feature = features(s)
        for half in range(2):
            wedge = wedge_of(feature, mine[half])
            where = (rows32(s), slice(half * 128, half * 128 + 128))
            wg[where] = wedge
            wlow[where] = wedge.astype(BF)
            wsq[where] = (wedge * wedge).astype(BF)

    over(0, NQ, weigh)

    db[...] = jnp.dot(oh[...], wsq[...], preferred_element_type=F32).astype(BF)
    denz[0]()
    dr[pl.ds(z, 1)] = db[rows32(z)][None]

    def half_sums(h):
        def weight(s):
            wedge = wg[rows32(s), h * 128 : h * 128 + 128]
            block = xb[h, s].astype(F32)
            wx[h, rows32(s), 0:128] = (wedge * block[:, 0:128]).astype(BF)
            wx[h, rows32(s), 128:256] = (wedge * block[:, 128:256]).astype(BF)

        over(0, NQ, weight)
        nb[h] = jnp.dot(oh[...], wx[h], preferred_element_type=F32).astype(BF)
        numz[h][0]()
        nr[h, pl.ds(z, 1)] = nb[h, rows32(z)][None]

    parts[0][1]()
    half_sums(0)

    refsz[1]()
    for plane in range(NZ):
        block = rr[plane].astype(F32)
        for k in range(NY):
            rf[k * 64 + plane * 8 : k * 64 + plane * 8 + 8, :] = block[8 * k : 8 * k + 8]
    for h in range(2):
        real = rf[:, h * 256 : h * 256 + 128]
        imag = rf[:, h * 256 + 128 : h * 256 + 256]
        rpow[:, h * 128 : h * 128 + 128] = (real * real + imag * imag).astype(BF)
    contract = (((1,), (1,)), ((), ()))
    sbe[...] = lax.dot_general(wlow[...], rpow[...], contract, preferred_element_type=F32).reshape(16, 2, 32, CLASSES)
    swap_e.start()
    part_sum = lax.dot_general(wx[0], rf[:, 0:256].astype(BF), contract, preferred_element_type=F32)
    sbi[...] = part_sum.reshape(16, 2, 32, CLASSES)

    parts[1][1]()
    half_sums(1)
    part_sum = lax.dot_general(wx[1], rf[:, 256:512].astype(BF), contract, preferred_element_type=F32)
    sbi[...] += part_sum.reshape(16, 2, 32, CLASSES)
    swap_i.start()

    stats[1]()
    s8[...] = jnp.sum(stb[...], axis=0)
    statz[0]()
    zs[pl.ds(z, 1)] = s8[...][None]

    swap_e.wait_recv()
    swap_i.wait_recv()

    def add_core(t):
        sm[t, 0] = (sbi[t, c] + pbi[t]).astype(BF)
        sm[t, 1] = (sbe[t, c] + pbe[t]).astype(BF)

    over(0, 16, add_core)
    backs[0]()
    b1[pl.ds(chip, 1)] = sm[pl.ds(chip, 1)]

    statz[1]()
    every = jnp.sum(zs[...], axis=0)
    count_ref[...] = every[0:1] * (CLASSES / PARTICLES)
    tcol[...] = jnp.zeros_like(tcol)
    tcol[0:2, :] = every
    pad0[...] = tcol[:, 0:128].T
    pad1[...] = tcol[:, 128:256].T

    denz[1]()
    denom = jnp.sum(dr[...].astype(F32), axis=0)
    tail = jnp.concatenate(
        [(pad0, pad1)[k // 2][pl.ds(pl.multiple_of((k % 2) * 64 + z * 8, 8), 8), 1:2] for k in range(NY)], axis=0
    )
    bottom = denom + TAU * (tail / COEF + 1.0)
    scale = 1.0 / bottom
    for h in range(2):
        numz[h][1]()
        top = jnp.sum(nr[h].astype(F32), axis=0)
        for part in range(2):
            lanes = slice(h * 128, h * 128 + 128)
            mb[:, part, lanes] = top[:, part * 128 : part * 128 + 128] * scale[:, lanes]
    means[0]()
    mr[pl.ds(q, 1)] = mb[pl.ds(q, 1)]

    backs[1]()
    inter = jnp.sum(b1[:, 0].astype(F32), axis=0)
    energy = jnp.sum(b1[:, 1].astype(F32), axis=0)
    score_ref[...] = inter / (
        math.sqrt(COEF) * jnp.sqrt((energy / COEF + EPS) * (power / COEF + EPS))
    )
    means[1]()
    for t in range(whole):
        mean_ref[0, :, t * WIDE : (t + 1) * WIDE] = mr[t]
    mean_ref[0, :, whole * WIDE : COEF] = mr[whole, :, 0:rest]
    for group in (mixed, *parts, stats, means, refsz, denz, *numz, statz, backs):
        group[2]()
    swap_e.wait_send()
    swap_i.wait_send()


def leave(score_in, mean_in, count_in, score_ref, mean_ref, count_ref, send):
    copies = [
        pltpu.make_async_copy(score_in, score_ref, send.at[0]),
        pltpu.make_async_copy(mean_in, mean_ref, send.at[1]),
        pltpu.make_async_copy(count_in, count_ref, send.at[2]),
    ]
    for copy in copies:
        copy.start()
    for copy in copies:
        copy.wait()


def body(particles, references, assignment, orientation, tilt_range):
    def v(*shape, dtype=F32):
        return pltpu.VMEM(shape, dtype)

    sem = pltpu.SemaphoreType.DMA
    vm = pl.BlockSpec(memory_space=pltpu.VMEM)
    hbm = pl.BlockSpec(memory_space=pltpu.HBM)
    shapes = (
        jax.ShapeDtypeStruct((PART, CLASSES), F32),
        jax.ShapeDtypeStruct((1, 2, COEF), F32),
        jax.ShapeDtypeStruct((1, CLASSES), F32),
    )
    outs = pl.pallas_call(
        kernel,
        out_shape=shapes,
        in_specs=[hbm] * 5,
        out_specs=(vm,) * 3,
        scratch_shapes=[
            v(PART, 2, COEF, dtype=BF), v(1, 2, COEF, dtype=BF),
            v(1, PART, dtype=jnp.int32), v(1, PART, dtype=jnp.int32), v(2, PART, dtype=jnp.int32),
            v(NQ, 4, WIDE, dtype=BF), v(NQ, 4, WIDE, dtype=BF),
            v(2, NQ, PART, WIDE, dtype=BF), v(2, NQ, PART, WIDE, dtype=BF),
            v(2, CLASSES), v(NQ, 2, CLASSES),
            v(32, 2 * WIDE, dtype=BF), v(NZ, 32, 2 * WIDE, dtype=BF),
            v(2, CLASSES, WIDE, dtype=BF), v(2, NZ, 32, WIDE, dtype=BF),
            v(CLASSES, WIDE, dtype=BF), v(NZ, 32, WIDE, dtype=BF),
            v(2, CLASSES), v(NZ, 2, CLASSES), v(128, CLASSES),
            v(128, 128), v(128, 128), v(5, 32, 128), v(32, 128),
            v(CLASSES, 1024, dtype=BF), v(1024, WIDE), v(1024, WIDE, dtype=BF), v(1024, WIDE, dtype=BF),
            v(2, 1024, WIDE, dtype=BF), v(CLASSES, 2 * WIDE), v(CLASSES, WIDE, dtype=BF),
            v(16, 2, 32, CLASSES), v(16, 2, 32, CLASSES), v(16, 32, CLASSES), v(16, 32, CLASSES),
            v(16, 2, 32, CLASSES, dtype=BF), v(16, 2, 32, CLASSES, dtype=BF), v(NQ, 2, WIDE), v(NQ, 2, WIDE),
        ] + [sem((2,)), sem((3,))] + [sem((2,))] * 4 + [sem] * 18,
        compiler_params=pltpu.CompilerParams(
            collective_id=0, has_side_effects=True
        ),
    )(particles, references, assignment.T, orientation[None], tilt_range)
    scores, means, counts = pl.pallas_call(
        leave, out_shape=shapes, in_specs=[vm] * 3, out_specs=(hbm,) * 3, scratch_shapes=[sem((3,))]
    )(*outs)
    return scores, means, counts[0]


def solution(mesh):
    split = Mesh(mesh.devices.reshape(NY, NZ, NX, NC), DOM)
    placed = (P(DOM, None, None), P(DOM, None, None), P(DOM, None), P(DOM), P(None, DOM))
    return jax.shard_map(
        body,
        mesh=split,
        in_specs=placed,
        out_specs=(P(DOM, None), P(DOM, None, None), P()),
        check_vma=False,
    )
```

time: 52.8 us -> 45.3 us (0.86)
  local copies, waits for them, and re-layouts: 4.43 us -> 0 us
  Pallas kernels: 47.5 us -> 44.5 us
    unnamed x11 -> x0, local copies, waits for them, and re-layouts: 3.23 us -> none
    pallas_call x1 -> x2, Pallas kernels: 47.5 us -> 44.5 us  [the longest x1 43 us: body(): pl.pallas_call(kernel, out_shape=shapes, in_specs=[hbm] * 5, out_specs=(v...]
    slice x2 -> x0, local copies, waits for them, and re-layouts: 1.19 us -> none  [the longest x1 0.63 us: body(): class_means = means.transpose(1, 0, 2).reshape(1, 2, padded)[:, :, :COEF]]
where the time goes in v3:
time: 45.3 us; the launch traced here: 45.1 us
  Pallas kernels  44.5 us (98%)
  between operations  0.64 us (1%)
    pallas_call x1, Pallas kernels, body(): pl.pallas_call(kernel, out_shape=shapes, in_specs=[hbm] * 5, out_specs=(v...  43 us
    pallas_call x1, Pallas kernels, body(): pl.pallas_call(leave, out_shape=shapes, in_specs=[vm] * 3, out_specs=(hbm...  1.49 us

profile of v3, /device:TPU:1, one launch (start us, length us, event | category | flops | bytes accessed | tf_op | source)
XLA Modules:
  0.0 45.1 jit_solution(17038125308317672986)
XLA Ops:
  0.6 43.0 %shard_map.76 = (f32[32,256]{1,0:T(8,128)}, f32[1,2,7488]{2,1,0:T(2,128)}, f32[1,256]{1,0:T(1,128)}) custom-call(bf16[32,2,7488]{2,1,0:T(2,128)(2,1)} %part_hbm.1, bf16[1,2,7488]{2,1,0:T(2,128)(2,1)} %ref_hbm.1, s32[1,32]{1,0:T(1,128)} %bitcast.3, s32[1,32]{1,0:T(1,128)} %bitcast.4, s32[2,32]{1,0:T(2,128)} %tilt_hbm.1), custom_call_target="tpu_custom_call" | custom-call | tf_op jit(solution)/shard_map/pallas_call | solution.py:404
  43.6 1.5 %shard_map.77 = (f32[32,256]{1,0:T(8,128)}, f32[1,2,7488]{2,1,0:T(2,128)}, f32[1,256]{1,0:T(1,128)}) custom-call(f32[32,256]{1,0:T(8,128)} %get-tuple-element.9.score_in, f32[1,2,7488]{2,1,0:T(2,128)} %get-tuple-element.10.mean_in, f32[1,256]{1,0:T(1,128)} %get-tuple-element.11.count_in), custom_call_target="tpu_custom_call" | custom-call | tf_op jit(solution)/shard_map/pallas_call | solution.py:429

commit v4 on v3

v4 whole, which is shorter than its diff:
```python
import math

import jax
import jax.numpy as jnp
from jax import lax
from jax.experimental import pallas as pl
from jax.experimental.pallas import tpu as pltpu
from jax.sharding import Mesh
from jax.sharding import PartitionSpec as P

GRID = 24
ORIENTS = 36
COEF = 7488
CLASSES = 256
PARTICLES = 8192
EPS = 1e-06
GAIN = 6.0
TAU = 0.5

NY, NZ, NX, NC = 4, 8, 4, 2
NQ = NY * NX * NC
PART = 32
WIDE = 256
TILE = 128
AROUND = (
    (2, 2), (1, 2), (3, 2), (2, 1), (2, 3), (0, 2), (2, 0),
    (1, 1), (3, 3), (1, 3), (3, 1), (0, 1), (0, 3), (1, 0), (3, 0),
)
SINGLE = (5, 12, 19, 26, 31)
DOM = ("y", "z", "x", "c")
BF = jnp.bfloat16
F32 = jnp.float32


def first_tile(q):
    return 2 * q - (q + 1) // 7


def frequencies(base, lanes=128):
    index = (lax.broadcasted_iota(jnp.int32, (1, lanes), 1) + base).astype(F32)
    plane = jnp.floor((index + 0.5) * (1.0 / (GRID * GRID)))
    rest = index - plane * (GRID * GRID)
    col_x = jnp.floor((rest + 0.5) * (1.0 / GRID))
    col_z = rest - col_x * GRID
    half = GRID // 2
    freq_x = jnp.where(col_x < half, col_x, col_x - GRID)
    freq_z = jnp.where(col_z < half, col_z, col_z - GRID)
    square_z = freq_z * freq_z
    return freq_x, plane, square_z, square_z + 1.0, -2.0 * freq_z, index


def wedge_of(feature, freq):
    sine, cosine, cos_centre, sin_centre, cos_width = feature
    freq_x, freq_y, square_z, square_z1, minus_2z, _ = freq
    along = freq_y * cosine - freq_x * sine
    square = along * along
    turned = ((square - square_z) * cos_centre + (minus_2z * along) * sin_centre) / (square + square_z1)
    return 1.0 / (1.0 + jnp.exp(-GAIN * (turned - cos_width)))


def kernel(
    part_hbm, ref_hbm, cls_hbm, ori_hbm, tilt_hbm,
    score_ref, mean_ref, count_ref,
    raw, rawr, lab_c, lab_o, lab_t, cm, cb, xs, xb, tm, tmr,
    r1, rr, nb, nr, db, dr, s8, zs,
    pad0, ft, sel, oh, wg, wlow, wsq, wx, rf, rpow,
    sbi, sbe, pbi, pbe, sm, b1, mb, mr,
    in_s, lab_s, x_s, x_r, nz_s, nz_r, b_s, b_r, c_s, c_r, t_s, t_r, m_s, m_r,
    rz_s, rz_r, dz_s, dz_r, sz_s, sz_r,
    pe_s, pe_r, pi_s, pi_r,
):
    y = lax.axis_index("y")
    z = lax.axis_index("z")
    x = lax.axis_index("x")
    c = lax.axis_index("c")
    q = y * 8 + x * 2 + c
    chip = y * 4 + x

    def to_chip(dy, dx, dc):
        ty, tx, tc = (y + dy) & 3, (x + dx) & 3, c ^ dc
        return (ty * 8 + tx * 2 + tc, ty * 4 + tx), {"y": ty, "z": z, "x": tx, "c": tc}

    def plane_peers():
        for dy, dx in AROUND:
            for dc in (0, 1):
                yield lambda dy=dy, dx=dx, dc=dc: to_chip(dy, dx, dc)
        yield lambda: to_chip(0, 0, 1)

    def chip_peers():
        for dy, dx in AROUND:
            yield lambda dy=dy, dx=dx: to_chip(dy, dx, 0)

    def z_peers():
        for d in (4, 3, 5, 2, 6, 1, 7):

            def peer(d=d):
                t = (z + d) & 7
                return (t, t), {"y": y, "z": t, "x": x, "c": c}

            yield peer

    other = {"y": y, "z": z, "x": x, "c": 1 - c}

    def over(first, last, step, unroll=1):
        def one(d, _):
            step(d)
            return 0

        lax.fori_loop(first, last, one, 0, unroll=unroll)

    def pair(t):
        return (t % 7 != 5) & (t != 31)

    def exchange(group, me, src, dst, blocks, send, recv, wants=None):
        peers, index = {"plane": (plane_peers, 0), "chip": (chip_peers, 1), "z": (z_peers, 0)}[group]

        def start():
            for peer in peers():
                ts, place = peer()
                t = ts[index]
                copy = pltpu.make_async_remote_copy(
                    src_ref=src(t), dst_ref=dst(me), send_sem=send, recv_sem=recv,
                    device_id=place, device_id_type=pl.DeviceIdType.MESH,
                )
                if wants is None:
                    copy.start()
                else:
                    pl.when(wants(t))(copy.start)

        def wait_recv():
            pltpu.make_async_copy(blocks, blocks, recv).wait()

        def wait_send():
            pltpu.make_async_copy(blocks, blocks, send).wait()

        return start, wait_recv, wait_send

    def rows32(t):
        return pl.ds(pl.multiple_of(t * 32, 32), 32)

    reads = [
        pltpu.make_async_copy(part_hbm, raw, in_s.at[0]),
        pltpu.make_async_copy(ref_hbm, rawr, in_s.at[1]),
        pltpu.make_async_copy(cls_hbm, lab_c, lab_s.at[0]),
        pltpu.make_async_copy(ori_hbm, lab_o, lab_s.at[1]),
        pltpu.make_async_copy(tilt_hbm, lab_t, lab_s.at[2]),
    ]
    for read in reads:
        read.start()

    barrier = pltpu.get_barrier_semaphore()

    for peers in (plane_peers, z_peers):
        for peer in peers():
            pl.semaphore_signal(barrier, inc=1, device_id=peer()[1], device_id_type=pl.DeviceIdType.MESH)

    few = pl.ds(0, NQ - 1)
    fewz = pl.ds(0, NZ - 1)
    mixed = exchange("plane", q, lambda t: cm.at[t], lambda s: cb.at[s], cb.at[few], c_s, c_r)

    def parts_of(h):
        return exchange(
            "plane", q, lambda t: xs.at[h, t], lambda s: xb.at[h, s], xb.at[h, few], x_s.at[h], x_r.at[h],
            pair if h else None,
        )

    parts = [parts_of(0), parts_of(1)]
    double = pair(q)

    def second_arrived():
        @pl.when(double)
        def _():
            parts[1][1]()

    def second_sent():
        for case, others in ((double, NQ - len(SINGLE) - 1), (jnp.logical_not(double), NQ - len(SINGLE))):

            @pl.when(case)
            def _():
                sent = xb.at[1, pl.ds(0, others)]
                pltpu.make_async_copy(sent, sent, x_s.at[1]).wait()

    totals = exchange("plane", q, lambda t: tm, lambda s: tmr.at[s], tmr.at[few], t_s, t_r)
    means = exchange("plane", q, lambda t: mb.at[t], lambda s: mr.at[s], mr.at[few], m_s, m_r)
    refsz = exchange("z", z, lambda t: r1, lambda s: rr.at[s], rr.at[fewz], rz_s, rz_r)
    denz = exchange("z", z, lambda t: db.at[rows32(t)], lambda s: dr.at[s], dr.at[fewz], dz_s, dz_r)

    def numz_of(h):
        return exchange(
            "z", z, lambda t: nb.at[h, rows32(t)], lambda s: nr.at[h, s], nr.at[h, fewz], nz_s.at[h], nz_r.at[h]
        )

    numz = [numz_of(0), numz_of(1)]
    statz = exchange("z", z, lambda t: s8, lambda s: zs.at[s], zs.at[fewz], sz_s, sz_r)

    def backs_of(k):
        return exchange(
            "chip", chip, lambda t: sm.at[k, t], lambda s: b1.at[k, s], b1.at[k, pl.ds(0, 15)], b_s.at[k], b_r.at[k]
        )

    backs = [backs_of(0), backs_of(1)]

    def to_other(src, dst, send, recv):
        return pltpu.make_async_remote_copy(
            src_ref=src.at[:, 1 - c], dst_ref=dst, send_sem=send, recv_sem=recv,
            device_id=other, device_id_type=pl.DeviceIdType.MESH,
        )

    swap_e = to_other(sbe, pbe, pe_s, pe_r)
    swap_i = to_other(sbi, pbi, pi_s, pi_r)

    for read in reads[2:]:
        read.wait()
    labels = jnp.concatenate([lab_c[...], lab_o[...], lab_t[0:1, :], lab_t[1:2, :]], axis=1).astype(F32)
    two_rows = jnp.concatenate([labels, jnp.zeros((1, 128), F32)], axis=0).astype(BF)
    cm[:, 2:4, 0:128] = jnp.broadcast_to(two_rows[None], (NQ, 2, 128))
    cm[:, 2:4, 128:256] = jnp.zeros((NQ, 2, 128), BF)
    reads[1].wait()
    for t in range(NQ):
        first = first_tile(t) * TILE
        size = min(TILE if t in SINGLE else WIDE, COEF - first)
        if size < WIDE:
            cm[t, 0:2, :] = jnp.zeros((2, WIDE), BF)
        cm[t, 0:2, 0:size] = rawr[0, :, first : first + size]

    reads[0].wait()

    for t in range(NQ):
        first = first_tile(t) * TILE
        size = min(TILE if t in SINGLE else WIDE, COEF - first)
        both = jnp.swapaxes(raw[:, :, first : first + size], 0, 1)
        for h in range(2):
            wide = min(TILE, size - h * TILE)
            if wide < TILE:
                xs[h, t] = jnp.zeros((PART, WIDE), BF)
            if wide > 0:
                for part in range(2):
                    xs[h, t, :, part * TILE : part * TILE + wide] = both[part, :, h * TILE : h * TILE + wide]
    pl.semaphore_wait(barrier, NQ - 1 + NZ - 1)

    mixed[0]()
    parts[0][0]()
    parts[1][0]()
    cb[pl.ds(q, 1)] = cm[pl.ds(q, 1)]

    @pl.when(jnp.logical_not(double))
    def _():
        xb[1] = jnp.zeros((NQ, PART, WIDE), BF)

    for h in range(2):
        xb[h, pl.ds(q, 1)] = xs[h, pl.ds(q, 1)]

    def features_of(turned):
        angle = turned[32:64] * (2.0 * math.pi / ORIENTS)
        low = -(40.0 + 1.5 * turned[64:96]) * (math.pi / 180.0)
        high = (40.0 + 1.5 * turned[96:128]) * (math.pi / 180.0)
        centre = low + high
        return jnp.sin(angle), jnp.cos(angle), jnp.cos(centre), jnp.sin(centre), jnp.cos(high - low)

    pad0[...] = jnp.broadcast_to(labels, (128, 128))
    own = features_of(pad0[...].T)

    def own_slice(s, power):
        for half in range(2):
            wedge = wedge_of(own, frequencies((first_tile(s) + half) * TILE))
            real = xs[half, s, :, 0:128].astype(F32)
            imag = xs[half, s, :, 128:256].astype(F32)
            power = power + wedge * (real * real + imag * imag)
        return power

    power = lax.fori_loop(0, NQ, own_slice, jnp.zeros((32, 128), F32), unroll=2)
    power = jnp.sum(power, axis=1, keepdims=True)

    mixed[1]()
    both = jnp.swapaxes(cb[:, 0:2, :], 0, 1)
    for h in range(2):
        for part in range(2):
            at = h * 256 + part * 128
            r1[:, at : at + 128] = both[part, :, h * 128 : h * 128 + 128]
    refsz[0]()
    rr[pl.ds(z, 1)] = r1[...][None]

    every = jnp.swapaxes(cb[:, 2:4, 0:128], 0, 1)[0].astype(F32)
    pad0[0:32, :] = every
    for k, feature in enumerate(features_of(pad0[...].T)):
        ft[k] = feature
    sub = lax.broadcasted_iota(jnp.int32, (32, 128), 0)
    cls = jnp.where(lax.broadcasted_iota(jnp.int32, (32, 128), 1) < 32, every, 0.0).astype(jnp.int32)
    in_plane = (((cls >> 3) & 7) * 32 + (cls >> 6) * 8 + (cls & 7)).astype(F32)
    chosen = in_plane
    for k in range(1, 4):
        chosen = jnp.where((sub & 3) == k, pltpu.roll(in_plane, 32 * k, 1), chosen)
    sel[...] = chosen
    class_row = lax.broadcasted_iota(jnp.int32, (CLASSES, 128), 0).astype(F32)
    for tile in range(8):
        row = jnp.sum(sel[4 * tile : 4 * tile + 4, :], axis=0, keepdims=True)
        oh[:, tile * 128 : tile * 128 + 128] = jnp.where(class_row == row, 1.0, 0.0).astype(BF)

    def features(s):
        index = jnp.full((32, 128), s, jnp.int32)
        return tuple(jnp.take_along_axis(ft[k], index, axis=1, mode="promise_in_bounds") for k in range(5))

    mine = [frequencies((first_tile(q) + h) * TILE) for h in range(2)]

    def weigh(s):
        feature = features(s)
        for half in range(2):
            wedge = wedge_of(feature, mine[half])
            where = (rows32(s), slice(half * 128, half * 128 + 128))
            wg[where] = wedge
            wlow[where] = wedge.astype(BF)
            wsq[where] = (wedge * wedge).astype(BF)

    over(0, NQ, weigh, unroll=2)

    contract = (((1,), (1,)), ((), ()))
    limits = (COEF, jnp.where(double, COEF, 0).astype(F32))
    valid = jnp.concatenate([jnp.where(mine[h][5] < limits[h], 1.0, 0.0) for h in range(2)], axis=1)
    valid = jnp.broadcast_to(valid, (8, WIDE)).astype(BF)
    total = lax.dot_general(valid, wlow[...], contract, preferred_element_type=F32)
    upper = total.astype(BF)
    rows = jnp.concatenate([jnp.ones((8, 1024), BF), upper, (total - upper.astype(F32)).astype(BF)], axis=0)
    found = lax.dot_general(rows, oh[...], contract, preferred_element_type=F32)
    s8[0:1] = found[0:1]
    s8[1:2] = found[8:9] + found[16:17]
    statz[0]()
    zs[pl.ds(z, 1)] = s8[...][None]

    db[...] = jnp.dot(oh[...], wsq[...], preferred_element_type=F32).astype(BF)
    denz[0]()
    dr[pl.ds(z, 1)] = db[rows32(z)][None]

    def weigh_half(h):
        def weight(s):
            wedge = wg[rows32(s), h * 128 : h * 128 + 128]
            block = xb[h, s].astype(F32)
            wx[h, rows32(s), 0:128] = (wedge * block[:, 0:128]).astype(BF)
            wx[h, rows32(s), 128:256] = (wedge * block[:, 128:256]).astype(BF)

        over(0, NQ, weight, unroll=4)

    def half_sums(h):
        nb[h] = jnp.dot(oh[...], wx[h], preferred_element_type=F32).astype(BF)
        numz[h][0]()
        nr[h, pl.ds(z, 1)] = nb[h, rows32(z)][None]

    def give_back(k, swap, mine, theirs):
        swap.wait_recv()

        def add_core(t):
            sm[k, t] = (mine[t, c] + theirs[t]).astype(BF)

        over(0, 16, add_core, unroll=4)
        backs[k][0]()
        b1[k, pl.ds(chip, 1)] = sm[k, pl.ds(chip, 1)]

    parts[0][1]()
    weigh_half(0)
    half_sums(0)

    refsz[1]()
    for plane in range(NZ):
        block = rr[plane].astype(F32)
        for k in range(NY):
            rf[k * 64 + plane * 8 : k * 64 + plane * 8 + 8, :] = block[8 * k : 8 * k + 8]
    for h in range(2):
        real = rf[:, h * 256 : h * 256 + 128]
        imag = rf[:, h * 256 + 128 : h * 256 + 256]
        rpow[:, h * 128 : h * 128 + 128] = (real * real + imag * imag).astype(BF)
    sbe[...] = lax.dot_general(wlow[...], rpow[...], contract, preferred_element_type=F32).reshape(16, 2, 32, CLASSES)
    swap_e.start()
    part_sum = lax.dot_general(wx[0], rf[:, 0:256].astype(BF), contract, preferred_element_type=F32)
    sbi[...] = part_sum.reshape(16, 2, 32, CLASSES)

    statz[1]()
    every = jnp.sum(zs[...], axis=0)
    here = every[1:2]
    tm[...] = jnp.where(z < 4, here[:, 0:128], here[:, 128:256])
    totals[0]()
    tmr[pl.ds(q, 1)] = tm[...][None]
    ids = lax.broadcasted_iota(jnp.int32, (CLASSES, CLASSES), 1)
    ids = ((ids >> 3) & 7) * 32 + (ids >> 6) * 8 + (ids & 7)
    order = jnp.where(lax.broadcasted_iota(jnp.int32, (CLASSES, CLASSES), 0) == ids, 1.0, 0.0).astype(BF)
    counts = jnp.broadcast_to(every[0:1], (8, CLASSES))
    upper = counts.astype(BF)
    rows = jnp.concatenate([upper, (counts - upper.astype(F32)).astype(BF)], axis=0)
    moved = jnp.dot(rows, order, preferred_element_type=F32)
    count_ref[...] = (moved[0:1] + moved[8:9]) * (CLASSES / PARTICLES)

    second_arrived()
    weigh_half(1)
    half_sums(1)
    part_sum = lax.dot_general(wx[1], rf[:, 256:512].astype(BF), contract, preferred_element_type=F32)
    sbi[...] += part_sum.reshape(16, 2, 32, CLASSES)
    swap_i.start()

    give_back(0, swap_e, sbe, pbe)
    give_back(1, swap_i, sbi, pbi)

    denz[1]()
    denom = jnp.sum(dr[...].astype(F32), axis=0)
    totals[1]()
    pad0[...] = jnp.broadcast_to(jnp.sum(tmr[...], axis=0), (128, 128)).T
    tail = pad0[pl.ds(pl.multiple_of((z % 4) * 32, 32), 32), 0:1]
    bottom = denom + TAU * (tail / COEF + 1.0)
    scale = 1.0 / bottom
    for h in range(2):
        numz[h][1]()
        top = jnp.sum(nr[h].astype(F32), axis=0)
        for part in range(2):
            lanes = slice(h * 128, h * 128 + 128)
            mb[:, part, lanes] = top[:, part * 128 : part * 128 + 128] * scale[:, lanes]
    means[0]()
    mr[pl.ds(q, 1)] = mb[pl.ds(q, 1)]

    backs[0][1]()
    energy = jnp.sum(b1[0].astype(F32), axis=0)
    backs[1][1]()
    inter = jnp.sum(b1[1].astype(F32), axis=0)
    score_ref[...] = inter / (
        math.sqrt(COEF) * jnp.sqrt((energy / COEF + EPS) * (power / COEF + EPS))
    )
    means[1]()
    for t in range(NQ):
        first = first_tile(t) * TILE
        size = min(TILE if t in SINGLE else WIDE, COEF - first)
        mean_ref[0, :, first : first + size] = mr[t, :, 0:size]
    for group in (mixed, parts[0], totals, means, refsz, denz, *numz, statz, *backs):
        group[2]()
    swap_e.wait_send()
    swap_i.wait_send()
    second_sent()


def leave(score_in, mean_in, count_in, score_ref, mean_ref, count_ref, send):
    copies = [
        pltpu.make_async_copy(score_in, score_ref, send.at[0]),
        pltpu.make_async_copy(mean_in, mean_ref, send.at[1]),
        pltpu.make_async_copy(count_in, count_ref, send.at[2]),
    ]
    for copy in copies:
        copy.start()
    for copy in copies:
        copy.wait()


def body(particles, references, assignment, orientation, tilt_range):
    def v(*shape, dtype=F32):
        return pltpu.VMEM(shape, dtype)

    sem = pltpu.SemaphoreType.DMA
    vm = pl.BlockSpec(memory_space=pltpu.VMEM)
    hbm = pl.BlockSpec(memory_space=pltpu.HBM)
    shapes = (
        jax.ShapeDtypeStruct((PART, CLASSES), F32),
        jax.ShapeDtypeStruct((1, 2, COEF), F32),
        jax.ShapeDtypeStruct((1, CLASSES), F32),
    )
    outs = pl.pallas_call(
        kernel,
        out_shape=shapes,
        in_specs=[hbm] * 5,
        out_specs=(vm,) * 3,
        scratch_shapes=[
            v(PART, 2, COEF, dtype=BF), v(1, 2, COEF, dtype=BF),
            v(1, PART, dtype=jnp.int32), v(1, PART, dtype=jnp.int32), v(2, PART, dtype=jnp.int32),
            v(NQ, 4, WIDE, dtype=BF), v(NQ, 4, WIDE, dtype=BF),
            v(2, NQ, PART, WIDE, dtype=BF), v(2, NQ, PART, WIDE, dtype=BF),
            v(1, 128), v(NQ, 1, 128),
            v(32, 2 * WIDE, dtype=BF), v(NZ, 32, 2 * WIDE, dtype=BF),
            v(2, CLASSES, WIDE, dtype=BF), v(2, NZ, 32, WIDE, dtype=BF),
            v(CLASSES, WIDE, dtype=BF), v(NZ, 32, WIDE, dtype=BF),
            v(2, CLASSES), v(NZ, 2, CLASSES),
            v(128, 128), v(5, 32, 128), v(32, 128),
            v(CLASSES, 1024, dtype=BF), v(1024, WIDE), v(1024, WIDE, dtype=BF), v(1024, WIDE, dtype=BF),
            v(2, 1024, WIDE, dtype=BF), v(CLASSES, 2 * WIDE), v(CLASSES, WIDE, dtype=BF),
            v(16, 2, 32, CLASSES), v(16, 2, 32, CLASSES), v(16, 32, CLASSES), v(16, 32, CLASSES),
            v(2, 16, 32, CLASSES, dtype=BF), v(2, 16, 32, CLASSES, dtype=BF), v(NQ, 2, WIDE), v(NQ, 2, WIDE),
        ] + [sem((2,)), sem((3,))] + [sem((2,))] * 6 + [sem] * 16,
        compiler_params=pltpu.CompilerParams(
            collective_id=0, has_side_effects=True
        ),
    )(particles, references, assignment.T, orientation[None], tilt_range)
    scores, means, counts = pl.pallas_call(
        leave, out_shape=shapes, in_specs=[vm] * 3, out_specs=(hbm,) * 3, scratch_shapes=[sem((3,))]
    )(*outs)
    return scores, means, counts[0]


def solution(mesh):
    split = Mesh(mesh.devices.reshape(NY, NZ, NX, NC), DOM)
    placed = (P(DOM, None, None), P(DOM, None, None), P(DOM, None), P(DOM), P(None, DOM))
    return jax.shard_map(
        body,
        mesh=split,
        in_specs=placed,
        out_specs=(P(DOM, None), P(DOM, None, None), P()),
        check_vma=False,
    )
```

time: 45.3 us -> 42.5 us (0.938)
  Pallas kernels: 44.5 us -> 41.7 us
    pallas_call x1, Pallas kernels: 43 us -> 40.2 us  [body(): pl.pallas_call(kernel, out_shape=shapes, in_specs=[hbm] * 5, out_specs=(v...]
where the time goes in v4:
time: 42.5 us; the launch traced here: 42.4 us
  Pallas kernels  41.7 us (98%)
  between operations  0.64 us (2%)
    pallas_call x1, Pallas kernels, body(): pl.pallas_call(kernel, out_shape=shapes, in_specs=[hbm] * 5, out_specs=(v...  40.2 us
    pallas_call x1, Pallas kernels, body(): pl.pallas_call(leave, out_shape=shapes, in_specs=[vm] * 3, out_specs=(hbm...  1.49 us

profile of v4, /device:TPU:1, one launch (start us, length us, event | category | flops | bytes accessed | tf_op | source)
XLA Modules:
  0.0 42.4 jit_solution(7241037705578892097)
XLA Ops:
  0.6 40.2 %shard_map.76 = (f32[32,256]{1,0:T(8,128)}, f32[1,2,7488]{2,1,0:T(2,128)}, f32[1,256]{1,0:T(1,128)}) custom-call(bf16[32,2,7488]{2,1,0:T(2,128)(2,1)} %part_hbm.1, bf16[1,2,7488]{2,1,0:T(2,128)(2,1)} %ref_hbm.1, s32[1,32]{1,0:T(1,128)} %bitcast.3, s32[1,32]{1,0:T(1,128)} %bitcast.4, s32[2,32]{1,0:T(2,128)} %tilt_hbm.1), custom_call_target="tpu_custom_call" | custom-call | tf_op jit(solution)/shard_map/pallas_call | solution.py:459
  40.9 1.5 %shard_map.77 = (f32[32,256]{1,0:T(8,128)}, f32[1,2,7488]{2,1,0:T(2,128)}, f32[1,256]{1,0:T(1,128)}) custom-call(f32[32,256]{1,0:T(8,128)} %get-tuple-element.9.score_in, f32[1,2,7488]{2,1,0:T(2,128)} %get-tuple-element.10.mean_in, f32[1,256]{1,0:T(1,128)} %get-tuple-element.11.count_in), custom_call_target="tpu_custom_call" | custom-call | tf_op jit(solution)/shard_map/pallas_call | solution.py:484

commit v5 on v4

--- a/solution.py
+++ b/solution.py
@@ -23,17 +23,18 @@
 WIDE = 256
 TILE = 128
 AROUND = (
-    (2, 2), (1, 2), (3, 2), (2, 1), (2, 3), (0, 2), (2, 0),
-    (1, 1), (3, 3), (1, 3), (3, 1), (0, 1), (0, 3), (1, 0), (3, 0),
+    (2, 2), (1, 1), (3, 3), (1, 2), (3, 2), (1, 3), (3, 1), (2, 1), (2, 3),
+    (0, 2), (2, 0), (0, 1), (1, 0), (0, 3), (3, 0),
 )
-SINGLE = (5, 12, 19, 26, 31)
+PADDED = 59 * TILE
+SINGLE = (1, 9, 17, 25, 31)
 DOM = ("y", "z", "x", "c")
 BF = jnp.bfloat16
 F32 = jnp.float32
 
 
 def first_tile(q):
-    return 2 * q - (q + 1) // 7
+    return 2 * q - (q + 6) // 8
 
 
 def frequencies(base, lanes=128):
@@ -64,8 +65,8 @@
     raw, rawr, lab_c, lab_o, lab_t, cm, cb, xs, xb, tm, tmr,
     r1, rr, nb, nr, db, dr, s8, zs,
     pad0, ft, sel, oh, wg, wlow, wsq, wx, rf, rpow,
-    sbi, sbe, pbi, pbe, sm, b1, mb, mr,
-    in_s, lab_s, x_s, x_r, nz_s, nz_r, b_s, b_r, c_s, c_r, t_s, t_r, m_s, m_r,
+    sbi, sbe, pbi, pbe, sm, b1, mb, sv, cv,
+    in_s, lab_s, out_s, x_s, x_r, nz_s, nz_r, b_s, b_r, c_s, c_r, t_s, t_r, m_s, m_r,
     rz_s, rz_r, dz_s, dz_r, sz_s, sz_r,
     pe_s, pe_r, pi_s, pi_r,
 ):
@@ -109,7 +110,7 @@
         lax.fori_loop(first, last, one, 0, unroll=unroll)
 
     def pair(t):
-        return (t % 7 != 5) & (t != 31)
+        return (t % 8 != 1) & (t != 31)
 
     def exchange(group, me, src, dst, blocks, send, recv, wants=None):
         peers, index = {"plane": (plane_peers, 0), "chip": (chip_peers, 1), "z": (z_peers, 0)}[group]
@@ -181,7 +182,30 @@
                 pltpu.make_async_copy(sent, sent, x_s.at[1]).wait()
 
     totals = exchange("plane", q, lambda t: tm, lambda s: tmr.at[s], tmr.at[few], t_s, t_r)
-    means = exchange("plane", q, lambda t: mb.at[t], lambda s: mr.at[s], mr.at[few], m_s, m_r)
+
+    def means_of(tiles):
+        lanes = pl.ds(pl.multiple_of(first_tile(q) * TILE, TILE), tiles * TILE)
+        inside = slice(0, tiles * TILE)
+        return (
+            exchange("plane", q, lambda t: mb.at[t, :, inside], lambda s: mean_ref.at[0, :, lanes], mb.at[few, :, inside], m_s, m_r),
+            pltpu.make_async_copy(mb.at[q, :, inside], mean_ref.at[0, :, lanes], out_s.at[2]),
+            mean_ref.at[0, :, 0 : PADDED - tiles * TILE],
+        )
+
+    def means(step):
+        for tiles, case in ((2, double), (1, jnp.logical_not(double))):
+
+            @pl.when(case)
+            def _():
+                others, own, expected = means_of(tiles)
+                if step == 0:
+                    others[0]()
+                    own.start()
+                else:
+                    pltpu.make_async_copy(expected, expected, m_r).wait()
+                    others[2]()
+                    own.wait()
+
     refsz = exchange("z", z, lambda t: r1, lambda s: rr.at[s], rr.at[fewz], rz_s, rz_r)
     denz = exchange("z", z, lambda t: db.at[rows32(t)], lambda s: dr.at[s], dr.at[fewz], dz_s, dz_r)
 
@@ -208,6 +232,8 @@
 
     swap_e = to_other(sbe, pbe, pe_s, pe_r)
     swap_i = to_other(sbi, pbi, pi_s, pi_r)
+    put_scores = pltpu.make_async_copy(sv, score_ref, out_s.at[0])
+    put_counts = pltpu.make_async_copy(cv, count_ref, out_s.at[1])
 
     for read in reads[2:]:
         read.wait()
@@ -369,9 +395,6 @@
         rpow[:, h * 128 : h * 128 + 128] = (real * real + imag * imag).astype(BF)
     sbe[...] = lax.dot_general(wlow[...], rpow[...], contract, preferred_element_type=F32).reshape(16, 2, 32, CLASSES)
     swap_e.start()
-    part_sum = lax.dot_general(wx[0], rf[:, 0:256].astype(BF), contract, preferred_element_type=F32)
-    sbi[...] = part_sum.reshape(16, 2, 32, CLASSES)
-
     statz[1]()
     every = jnp.sum(zs[...], axis=0)
     here = every[1:2]
@@ -385,16 +408,19 @@
     upper = counts.astype(BF)
     rows = jnp.concatenate([upper, (counts - upper.astype(F32)).astype(BF)], axis=0)
     moved = jnp.dot(rows, order, preferred_element_type=F32)
-    count_ref[...] = (moved[0:1] + moved[8:9]) * (CLASSES / PARTICLES)
+    cv[...] = (moved[0:1] + moved[8:9]) * (CLASSES / PARTICLES)
+    put_counts.start()
 
     second_arrived()
     weigh_half(1)
     half_sums(1)
-    part_sum = lax.dot_general(wx[1], rf[:, 256:512].astype(BF), contract, preferred_element_type=F32)
-    sbi[...] += part_sum.reshape(16, 2, 32, CLASSES)
+
+    give_back(0, swap_e, sbe, pbe)
+
+    part_sum = lax.dot_general(wx[0], rf[:, 0:256].astype(BF), contract, preferred_element_type=F32)
+    part_sum = part_sum + lax.dot_general(wx[1], rf[:, 256:512].astype(BF), contract, preferred_element_type=F32)
+    sbi[...] = part_sum.reshape(16, 2, 32, CLASSES)
     swap_i.start()
-
-    give_back(0, swap_e, sbe, pbe)
     give_back(1, swap_i, sbi, pbi)
 
     denz[1]()
@@ -410,38 +436,30 @@
         for part in range(2):
             lanes = slice(h * 128, h * 128 + 128)
             mb[:, part, lanes] = top[:, part * 128 : part * 128 + 128] * scale[:, lanes]
-    means[0]()
-    mr[pl.ds(q, 1)] = mb[pl.ds(q, 1)]
+    means(0)
 
     backs[0][1]()
     energy = jnp.sum(b1[0].astype(F32), axis=0)
     backs[1][1]()
     inter = jnp.sum(b1[1].astype(F32), axis=0)
-    score_ref[...] = inter / (
+    sv[...] = inter / (
         math.sqrt(COEF) * jnp.sqrt((energy / COEF + EPS) * (power / COEF + EPS))
     )
-    means[1]()
-    for t in range(NQ):
-        first = first_tile(t) * TILE
-        size = min(TILE if t in SINGLE else WIDE, COEF - first)
-        mean_ref[0, :, first : first + size] = mr[t, :, 0:size]
-    for group in (mixed, parts[0], totals, means, refsz, denz, *numz, statz, *backs):
+    put_scores.start()
+    means(1)
+    for leaving in (put_counts, put_scores):
+        leaving.wait()
+    for group in (mixed, parts[0], totals, refsz, denz, *numz, statz, *backs):
         group[2]()
     swap_e.wait_send()
     swap_i.wait_send()
     second_sent()
 
 
-def leave(score_in, mean_in, count_in, score_ref, mean_ref, count_ref, send):
-    copies = [
-        pltpu.make_async_copy(score_in, score_ref, send.at[0]),
-        pltpu.make_async_copy(mean_in, mean_ref, send.at[1]),
-        pltpu.make_async_copy(count_in, count_ref, send.at[2]),
-    ]
-    for copy in copies:
-        copy.start()
-    for copy in copies:
-        copy.wait()
+def leave(score_in, mean_in, count_in, score_ref, mean_ref, count_ref):
+    score_ref[...] = score_in[...]
+    mean_ref[...] = mean_in[:, :, 0:COEF]
+    count_ref[...] = count_in[...]
 
 
 def body(particles, references, assignment, orientation, tilt_range):
@@ -451,16 +469,18 @@
     sem = pltpu.SemaphoreType.DMA
     vm = pl.BlockSpec(memory_space=pltpu.VMEM)
     hbm = pl.BlockSpec(memory_space=pltpu.HBM)
-    shapes = (
-        jax.ShapeDtypeStruct((PART, CLASSES), F32),
-        jax.ShapeDtypeStruct((1, 2, COEF), F32),
-        jax.ShapeDtypeStruct((1, CLASSES), F32),
-    )
+    def shapes(wide):
+        return (
+            jax.ShapeDtypeStruct((PART, CLASSES), F32),
+            jax.ShapeDtypeStruct((1, 2, wide), F32),
+            jax.ShapeDtypeStruct((1, CLASSES), F32),
+        )
+
     outs = pl.pallas_call(
         kernel,
-        out_shape=shapes,
+        out_shape=shapes(PADDED),
         in_specs=[hbm] * 5,
-        out_specs=(vm,) * 3,
+        out_specs=(hbm,) * 3,
         scratch_shapes=[
             v(PART, 2, COEF, dtype=BF), v(1, 2, COEF, dtype=BF),
             v(1, PART, dtype=jnp.int32), v(1, PART, dtype=jnp.int32), v(2, PART, dtype=jnp.int32),
@@ -475,14 +495,14 @@
             v(CLASSES, 1024, dtype=BF), v(1024, WIDE), v(1024, WIDE, dtype=BF), v(1024, WIDE, dtype=BF),
             v(2, 1024, WIDE, dtype=BF), v(CLASSES, 2 * WIDE), v(CLASSES, WIDE, dtype=BF),
             v(16, 2, 32, CLASSES), v(16, 2, 32, CLASSES), v(16, 32, CLASSES), v(16, 32, CLASSES),
-            v(2, 16, 32, CLASSES, dtype=BF), v(2, 16, 32, CLASSES, dtype=BF), v(NQ, 2, WIDE), v(NQ, 2, WIDE),
-        ] + [sem((2,)), sem((3,))] + [sem((2,))] * 6 + [sem] * 16,
+            v(2, 16, 32, CLASSES, dtype=BF), v(2, 16, 32, CLASSES, dtype=BF), v(NQ, 2, WIDE), v(PART, CLASSES), v(1, CLASSES),
+        ] + [sem((2,)), sem((3,)), sem((3,))] + [sem((2,))] * 6 + [sem] * 16,
         compiler_params=pltpu.CompilerParams(
             collective_id=0, has_side_effects=True
         ),
     )(particles, references, assignment.T, orientation[None], tilt_range)
     scores, means, counts = pl.pallas_call(
-        leave, out_shape=shapes, in_specs=[vm] * 3, out_specs=(hbm,) * 3, scratch_shapes=[sem((3,))]
+        leave, out_shape=shapes(COEF), in_specs=[vm] * 3, out_specs=(vm,) * 3
     )(*outs)
     return scores, means, counts[0]
 

time: 42.5 us -> 40.9 us (0.962)
  Pallas kernels: 41.7 us -> 40.2 us
    pallas_call x2, Pallas kernels: 41.7 us -> 40.2 us  [the longest x1 38.7 us: body(): pl.pallas_call(kernel, out_shape=shapes(PADDED), in_specs=[hbm] * 5, out_...]
where the time goes in v5:
time: 40.9 us; the launch traced here: 40.8 us
  Pallas kernels  40.2 us (98%)
  between operations  0.64 us (2%)
    pallas_call x1, Pallas kernels, body(): pl.pallas_call(kernel, out_shape=shapes(PADDED), in_specs=[hbm] * 5, out_...  38.7 us
    pallas_call x1, Pallas kernels, body(): pl.pallas_call(leave, out_shape=shapes(COEF), in_specs=[vm] * 3, out_spec...  1.47 us

profile of v5, /device:TPU:1, one launch (start us, length us, event | category | flops | bytes accessed | tf_op | source)
XLA Modules:
  0.0 40.8 jit_solution(7222366662720057404)
XLA Ops:
  0.6 38.7 %shard_map.76 = (f32[32,256]{1,0:T(8,128)}, f32[1,2,7552]{2,1,0:T(2,128)}, f32[1,256]{1,0:T(1,128)}) custom-call(bf16[32,2,7488]{2,1,0:T(2,128)(2,1)} %part_hbm.1, bf16[1,2,7488]{2,1,0:T(2,128)(2,1)} %ref_hbm.1, s32[1,32]{1,0:T(1,128)} %bitcast.3, s32[1,32]{1,0:T(1,128)} %bitcast.4, s32[2,32]{1,0:T(2,128)} %tilt_hbm.1), custom_call_target="tpu_custom_call" | custom-call | tf_op jit(solution)/shard_map/pallas_call | solution.py:479
  39.3 1.5 %shard_map.77 = (f32[32,256]{1,0:T(8,128)}, f32[1,2,7488]{2,1,0:T(2,128)}, f32[1,256]{1,0:T(1,128)}) custom-call(f32[32,256]{1,0:T(8,128)} %get-tuple-element.9.score_in, f32[1,2,7552]{2,1,0:T(2,128)} %get-tuple-element.10.mean_in, f32[1,256]{1,0:T(1,128)} %get-tuple-element.11.count_in), custom_call_target="tpu_custom_call" | custom-call | tf_op jit(solution)/shard_map/pallas_call | solution.py:504

commit v6 on v5

--- a/solution.py
+++ b/solution.py
@@ -22,9 +22,12 @@
 PART = 32
 WIDE = 256
 TILE = 128
-AROUND = (
+OUTER = (
     (2, 2), (1, 1), (3, 3), (1, 2), (3, 2), (1, 3), (3, 1), (2, 1), (2, 3),
     (0, 2), (2, 0), (0, 1), (1, 0), (0, 3), (3, 0),
+)
+AROUND = (
+    (0, 3), (0, 1), (3, 3), (1, 1), (3, 2), (1, 2), (2, 2), (1, 0), (3, 0), (2, 1), (2, 3), (2, 0), (0, 2), (1, 3), (3, 1),
 )
 PADDED = 59 * TILE
 SINGLE = (1, 9, 17, 25, 31)
@@ -81,14 +84,14 @@
         ty, tx, tc = (y + dy) & 3, (x + dx) & 3, c ^ dc
         return (ty * 8 + tx * 2 + tc, ty * 4 + tx), {"y": ty, "z": z, "x": tx, "c": tc}
 
-    def plane_peers():
-        for dy, dx in AROUND:
+    def plane_peers(around=AROUND):
+        for dy, dx in around:
             for dc in (0, 1):
                 yield lambda dy=dy, dx=dx, dc=dc: to_chip(dy, dx, dc)
         yield lambda: to_chip(0, 0, 1)
 
-    def chip_peers():
-        for dy, dx in AROUND:
+    def chip_peers(around=AROUND):
+        for dy, dx in around:
             yield lambda dy=dy, dx=dx: to_chip(dy, dx, 0)
 
     def z_peers():
@@ -112,11 +115,11 @@
     def pair(t):
         return (t % 8 != 1) & (t != 31)
 
-    def exchange(group, me, src, dst, blocks, send, recv, wants=None):
+    def exchange(group, me, src, dst, blocks, send, recv, wants=None, around=AROUND):
         peers, index = {"plane": (plane_peers, 0), "chip": (chip_peers, 1), "z": (z_peers, 0)}[group]
 
         def start():
-            for peer in peers():
+            for peer in peers(*(() if group == "z" else (around,))):
                 ts, place = peer()
                 t = ts[index]
                 copy = pltpu.make_async_remote_copy(
@@ -187,7 +190,7 @@
         lanes = pl.ds(pl.multiple_of(first_tile(q) * TILE, TILE), tiles * TILE)
         inside = slice(0, tiles * TILE)
         return (
-            exchange("plane", q, lambda t: mb.at[t, :, inside], lambda s: mean_ref.at[0, :, lanes], mb.at[few, :, inside], m_s, m_r),
+            exchange("plane", q, lambda t: mb.at[t, :, inside], lambda s: mean_ref.at[0, :, lanes], mb.at[few, :, inside], m_s, m_r, None, OUTER),
             pltpu.make_async_copy(mb.at[q, :, inside], mean_ref.at[0, :, lanes], out_s.at[2]),
             mean_ref.at[0, :, 0 : PADDED - tiles * TILE],
         )
@@ -219,7 +222,7 @@
 
     def backs_of(k):
         return exchange(
-            "chip", chip, lambda t: sm.at[k, t], lambda s: b1.at[k, s], b1.at[k, pl.ds(0, 15)], b_s.at[k], b_r.at[k]
+            "chip", chip, lambda t: sm.at[k, t], lambda s: b1.at[k, s], b1.at[k, pl.ds(0, 15)], b_s.at[k], b_r.at[k], None, OUTER
         )
 
     backs = [backs_of(0), backs_of(1)]
@@ -411,11 +414,11 @@
     cv[...] = (moved[0:1] + moved[8:9]) * (CLASSES / PARTICLES)
     put_counts.start()
 
+    give_back(0, swap_e, sbe, pbe)
     second_arrived()
     weigh_half(1)
     half_sums(1)
 
-    give_back(0, swap_e, sbe, pbe)
 
     part_sum = lax.dot_general(wx[0], rf[:, 0:256].astype(BF), contract, preferred_element_type=F32)
     part_sum = part_sum + lax.dot_general(wx[1], rf[:, 256:512].astype(BF), contract, preferred_element_type=F32)

time: 40.9 us -> 40.5 us (level)
  Pallas kernels: 40.2 us -> 39.7 us
    pallas_call x1, Pallas kernels: 38.7 us -> 38.3 us  [body(): pl.pallas_call(kernel, out_shape=shapes(PADDED), in_specs=[hbm] * 5, out_...]
where the time goes in v6:
time: 40.5 us; the launch traced here: 40.4 us
  Pallas kernels  39.7 us (98%)
  between operations  0.64 us (2%)
    pallas_call x1, Pallas kernels, body(): pl.pallas_call(kernel, out_shape=shapes(PADDED), in_specs=[hbm] * 5, out_...  38.3 us
    pallas_call x1, Pallas kernels, body(): pl.pallas_call(leave, out_shape=shapes(COEF), in_specs=[vm] * 3, out_spec...  1.47 us

profile of v6, /device:TPU:1, one launch (start us, length us, event | category | flops | bytes accessed | tf_op | source)
XLA Modules:
  0.0 40.4 jit_solution(15634880591722910865)
XLA Ops:
  0.6 38.3 %shard_map.76 = (f32[32,256]{1,0:T(8,128)}, f32[1,2,7552]{2,1,0:T(2,128)}, f32[1,256]{1,0:T(1,128)}) custom-call(bf16[32,2,7488]{2,1,0:T(2,128)(2,1)} %part_hbm.1, bf16[1,2,7488]{2,1,0:T(2,128)(2,1)} %ref_hbm.1, s32[1,32]{1,0:T(1,128)} %bitcast.3, s32[1,32]{1,0:T(1,128)} %bitcast.4, s32[2,32]{1,0:T(2,128)} %tilt_hbm.1), custom_call_target="tpu_custom_call" | custom-call | tf_op jit(solution)/shard_map/pallas_call | solution.py:482
  38.9 1.5 %shard_map.77 = (f32[32,256]{1,0:T(8,128)}, f32[1,2,7488]{2,1,0:T(2,128)}, f32[1,256]{1,0:T(1,128)}) custom-call(f32[32,256]{1,0:T(8,128)} %get-tuple-element.9.score_in, f32[1,2,7552]{2,1,0:T(2,128)} %get-tuple-element.10.mean_in, f32[1,256]{1,0:T(1,128)} %get-tuple-element.11.count_in), custom_call_target="tpu_custom_call" | custom-call | tf_op jit(solution)/shard_map/pallas_call | solution.py:507

commit v7 on v6

--- a/solution.py
+++ b/solution.py
@@ -356,8 +356,6 @@
     zs[pl.ds(z, 1)] = s8[...][None]
 
     db[...] = jnp.dot(oh[...], wsq[...], preferred_element_type=F32).astype(BF)
-    denz[0]()
-    dr[pl.ds(z, 1)] = db[rows32(z)][None]
 
     def weigh_half(h):
         def weight(s):
@@ -366,7 +364,7 @@
             wx[h, rows32(s), 0:128] = (wedge * block[:, 0:128]).astype(BF)
             wx[h, rows32(s), 128:256] = (wedge * block[:, 128:256]).astype(BF)
 
-        over(0, NQ, weight, unroll=4)
+        over(0, NQ, weight, unroll=8)
 
     def half_sums(h):
         nb[h] = jnp.dot(oh[...], wx[h], preferred_element_type=F32).astype(BF)
@@ -379,13 +377,15 @@
         def add_core(t):
             sm[k, t] = (mine[t, c] + theirs[t]).astype(BF)
 
-        over(0, 16, add_core, unroll=4)
+        over(0, 16, add_core, unroll=8)
         backs[k][0]()
         b1[k, pl.ds(chip, 1)] = sm[k, pl.ds(chip, 1)]
 
     parts[0][1]()
     weigh_half(0)
     half_sums(0)
+    denz[0]()
+    dr[pl.ds(z, 1)] = db[rows32(z)][None]
 
     refsz[1]()
     for plane in range(NZ):

time: 40.5 us -> 40.5 us (level)
  no operation moved by 1% of the time
where the time goes in v7:
time: 40.5 us; the launch traced here: 40.3 us
  Pallas kernels  39.7 us (98%)
  between operations  0.64 us (2%)
    pallas_call x1, Pallas kernels, body(): pl.pallas_call(kernel, out_shape=shapes(PADDED), in_specs=[hbm] * 5, out_...  38.2 us
    pallas_call x1, Pallas kernels, body(): pl.pallas_call(leave, out_shape=shapes(COEF), in_specs=[vm] * 3, out_spec...  1.47 us

profile of v7, /device:TPU:1, one launch (start us, length us, event | category | flops | bytes accessed | tf_op | source)
XLA Modules:
  0.0 40.3 jit_solution(13842547958195606357)
XLA Ops:
  0.6 38.2 %shard_map.76 = (f32[32,256]{1,0:T(8,128)}, f32[1,2,7552]{2,1,0:T(2,128)}, f32[1,256]{1,0:T(1,128)}) custom-call(bf16[32,2,7488]{2,1,0:T(2,128)(2,1)} %part_hbm.1, bf16[1,2,7488]{2,1,0:T(2,128)(2,1)} %ref_hbm.1, s32[1,32]{1,0:T(1,128)} %bitcast.3, s32[1,32]{1,0:T(1,128)} %bitcast.4, s32[2,32]{1,0:T(2,128)} %tilt_hbm.1), custom_call_target="tpu_custom_call" | custom-call | tf_op jit(solution)/shard_map/pallas_call | solution.py:482
  38.9 1.5 %shard_map.77 = (f32[32,256]{1,0:T(8,128)}, f32[1,2,7488]{2,1,0:T(2,128)}, f32[1,256]{1,0:T(1,128)}) custom-call(f32[32,256]{1,0:T(8,128)} %get-tuple-element.9.score_in, f32[1,2,7552]{2,1,0:T(2,128)} %get-tuple-element.10.mean_in, f32[1,256]{1,0:T(1,128)} %get-tuple-element.11.count_in), custom_call_target="tpu_custom_call" | custom-call | tf_op jit(solution)/shard_map/pallas_call | solution.py:507
